TPU v7x, 32 devices: a whole 2x2x4 slice. The times are simulated.
32 devices in a mesh: tm: 4 (over z), paths: 8 (over y, x, core).
Axes of the slice: x: 2, y: 2, z: 4, core: 2. Of those that a mesh axis runs over, the one named last changes fastest.
Arguments:
- start_curve: float32 [80], replicated, may hold values from 0.02 to 0.06
- loadings: float32 [4, 80], replicated, may hold values from 0.2 to 1
- vols: float32 [40, 80], P('tm'), may hold values from 0.08 to 0.4
- shocks: float32 [40, 4, 16384], P('tm', None, 'paths'), may hold values from -5 to 5
- exercise_bits: int32 [40, 16384], P('tm', 'paths'), may hold values 0 or 1
- regress: float32 [40, 6], P('tm'), may hold values from -0.03 to 0.03
- date_slot: int32 [40], P('tm'), may hold values from 0 to 39, each once
- ck_rates: float32 [4, 80, 16384], P('tm', None, 'paths'), may hold values from 0.02 to 0.07
- ck_numer: float32 [4, 16384], P('tm', 'paths'), may hold values from 1 to 3
- ck_survive: float32 [4, 16384], P('tm', 'paths'), may hold values from 0.2 to 1
Outputs:
- vega: float32 [40, 80], P('tm')
- path_value: float32 [16384], P('paths')
Inputs may be any that keep to these rules, and one draw needn't show every extreme that they name: `date_slot`: each row of regress is named once: a permutation of the 40 rows.
All inputs are finite; a program needn't handle non-finite values. No bound on the sum of `exercise_bits` on one device may be relied on, other than what follows from the above.
Results may differ from a plain program's by a relative error of at most 0.0003.
Values sent between devices are 32-bit elements; how exact they have to be, the bound alone decides.
No kernel may reach another device: no remote copies, remote signals or barrier semaphores. Data moves between devices by JAX's collectives and lax.ppermute only.
A program may use at most 128 MiB of HBM per device.

v0:
```python
import jax
import jax.numpy as jnp
from jax import lax
from jax.sharding import PartitionSpec as P

ACCRUAL = 0.25
STRIKE = 0.04
SMOOTHING = 0.01
NOTIONAL = 100.0
HIGHEST = lax.Precision.HIGHEST


def passed_along(value, axis, steps):
    count = lax.axis_size(axis)
    initial, last = (max(0, -steps), min(count, count - steps))
    return lax.ppermute(value, axis, [(source, source + steps) for source in range(initial, last)])


def segment(
    rates_in,
    numeraire,
    survival,
    vol_rows,
    shock_rows,
    flag_rows,
    weight_rows,
    loadings,
    first_date,
):
    forwards = rates_in.shape[0]
    positions = jnp.arange(forwards, dtype=jnp.int32)
    triangle = (positions[:, None] >= positions[None, :]).astype(jnp.float32)
    factor_loads = loadings / jnp.sqrt(jnp.sum(loadings * loadings, axis=0, keepdims=True))
    current = rates_in
    path_total = jnp.zeros(numeraire.shape, jnp.float32)
    for offset_date in range(vol_rows.shape[0]):
        date_index = first_date + offset_date
        opening = 2 * date_index + 1
        earlier = jnp.where(date_index == 0, 0, 2 * date_index - 1)
        horizon = jnp.where(date_index == 0, ACCRUAL, 2.0 * ACCRUAL)
        growth = jnp.log1p(ACCRUAL * current)
        fixing = ((positions >= earlier) & (positions < opening)).astype(jnp.float32)
        numeraire = numeraire * jnp.exp(jnp.sum(fixing[:, None] * growth, axis=0))
        living = (positions >= opening).astype(jnp.float32)
        sigma = vol_rows[offset_date] * living
        scaled = ACCRUAL * current * sigma[:, None] / (1.0 + ACCRUAL * current)
        running = jnp.einsum(
            "ij,fjp->fip", triangle, factor_loads[:, :, None] * scaled[None], precision=HIGHEST
        )
        drift = sigma[:, None] * jnp.sum(factor_loads[:, :, None] * running, axis=0)
        noise = jnp.einsum("fi,fp->ip", factor_loads, shock_rows[offset_date], precision=HIGHEST)
        exponent = (
            horizon * drift
            - 0.5 * horizon * (sigma * sigma)[:, None]
            + jnp.sqrt(horizon) * sigma[:, None] * noise
        )
        current = current * jnp.exp(exponent)
        discount = jnp.dot(
            triangle, living[:, None] * jnp.log1p(ACCRUAL * current), precision=HIGHEST
        )
        bonds = jnp.exp(-discount)
        annuity = ACCRUAL * jnp.sum(living[:, None] * bonds, axis=0)
        floating = 1.0 - bonds[forwards - 1]
        exercise = floating - STRIKE * annuity
        moneyness = (floating / annuity - STRIKE) / SMOOTHING
        basis = jnp.stack(
            [
                jnp.ones_like(moneyness),
                moneyness,
                moneyness * moneyness,
                annuity,
                annuity * moneyness,
                annuity * moneyness * moneyness,
            ]
        )
        continuation = jnp.einsum("b,bp->p", weight_rows[offset_date], basis, precision=HIGHEST)
        chance = flag_rows[offset_date] * jax.nn.sigmoid((exercise - continuation) / SMOOTHING)
        path_total = path_total + NOTIONAL * survival * chance * exercise / numeraire
        survival = survival * (1.0 - chance)
    return (current, numeraire, survival, path_total)


def pullback(
    opening_state,
    vol_rows,
    shock_rows,
    flag_rows,
    weight_rows,
    loadings,
    first_date,
    adjoint_in,
    path_weight,
):

    def runner(rates_in, numer_in, survive_in, local_vols):
        return segment(
            rates_in,
            numer_in,
            survive_in,
            local_vols,
            shock_rows,
            flag_rows,
            weight_rows,
            loadings,
            first_date,
        )

    outputs, reverse_map = jax.vjp(
        runner, opening_state[0], opening_state[1], opening_state[2], vol_rows
    )
    gradient = reverse_map(
        (adjoint_in[0], adjoint_in[1], adjoint_in[2], jnp.full_like(outputs[3], path_weight))
    )
    return ((gradient[0], gradient[1], gradient[2]), gradient[3], outputs[3])


def add_values(partial_values):
    return lax.psum(partial_values, "tm")


def local(
    start_curve,
    loadings,
    vols,
    shocks,
    exercise_bits,
    regress,
    date_slot,
    ck_rates,
    ck_numer,
    ck_survive,
):
    shard_count = lax.axis_size("tm")
    group_count = lax.axis_size("paths")
    device_index = lax.axis_index("tm")
    per_shard = vols.shape[0]
    path_count = shocks.shape[2]
    forwards = vols.shape[1]
    date_count = per_shard * shard_count
    path_weight = NOTIONAL / (path_count * group_count)
    table = lax.all_gather(regress, "tm", axis=0, tiled=True)
    onehot = (date_slot[:, None] == jnp.arange(date_count, dtype=jnp.int32)[None, :]).astype(
        jnp.float32
    )
    weight_rows = jnp.dot(onehot, table, precision=HIGHEST)
    flag_rows = exercise_bits.astype(jnp.float32)
    received = passed_along((ck_rates[0], ck_numer[0], ck_survive[0]), "tm", 1)
    is_first = device_index == 0
    opening_state = (
        jnp.where(is_first, start_curve[:, None], received[0]),
        jnp.where(is_first, 1.0, received[1]),
        jnp.where(is_first, 1.0, received[2]),
    )
    first_date = device_index * per_shard
    zero_adjoint = (
        jnp.zeros((forwards, path_count), jnp.float32),
        jnp.zeros((path_count,), jnp.float32),
        jnp.zeros((path_count,), jnp.float32),
    )

    def take_turn(turn_index, loop_state):
        incoming, vega_total, chain_values = loop_state
        active = device_index == shard_count - 1 - turn_index

        def do_pullback(adjoint_in):
            return pullback(
                opening_state,
                vols,
                shocks,
                flag_rows,
                weight_rows,
                loadings,
                first_date,
                adjoint_in,
                path_weight,
            )

        def do_nothing(adjoint_in):
            return (zero_adjoint, jnp.zeros_like(vols), jnp.zeros((path_count,), jnp.float32))

        outgoing, turn_vega, turn_values = lax.cond(active, do_pullback, do_nothing, incoming)
        passed = passed_along(outgoing, "tm", -1)
        return (passed, vega_total + turn_vega, chain_values + turn_values)

    initial_state = (zero_adjoint, jnp.zeros_like(vols), jnp.zeros((path_count,), jnp.float32))
    final_state = lax.fori_loop(0, shard_count, take_turn, initial_state)
    vega_part = final_state[1]
    chain_values = final_state[2]
    path_value = add_values(chain_values)
    vega = lax.psum(vega_part, "paths")
    return (vega, path_value)


def solution(mesh):
    return jax.shard_map(
        local,
        mesh=mesh,
        in_specs=(
            P(),
            P(),
            P("tm", None),
            P("tm", None, "paths"),
            P("tm", "paths"),
            P("tm", None),
            P("tm"),
            P("tm", None, "paths"),
            P("tm", "paths"),
            P("tm", "paths"),
        ),
        out_specs=(P("tm", None), P("paths")),
        check_vma=False,
    )
```

profile of v0, /device:TPU:0, one launch (start us, length us, event | category | flops | bytes accessed | tf_op | source)
XLA Modules:
  0.0 764.6 jit_solution(1220276577194801773)
XLA Ops:
  0.6 5.0 collective-permute-start.3
  5.6 3.4 collective-permute-start.4
  9.1 3.5 collective-permute-start.5
  12.6 16.0 %all-gather = f32[4,10,6]{1,2,0:T(8,128)S(1)} all-gather(f32[1,10,6]{1,2,0:T(8,128)} %bitcast.998), channel_id=1, replica_groups=mesh['tm'=4,'paths'=8] {'tm'}, dimensions={0}, use_global_device_ids=true | all-gather | bytes 1200 | tf_op jit(solution)/shard_map/all_gather | solution.py:141
  36.0 706.4 %while.22 = (s32[]{:T(128)}, f32[80,2048]{1,0:T(8,128)}, f32[2048]{0:T(1024)}, f32[2048]{0:T(1024)}, f32[10,80]{1,0:T(8,128)}, /*index=5*/f32[2048]{0:T(1024)}, ...) while((s32[]{:T(128)}, f32[80,2048]{1,0:T(8,128)}, ...), condition=%wide.region_84.85_spmd.clone, body=%wide.region_0.84_spmd.clone.sunk | while | flops 15945723904 | bytes 387224288 | solution.py:186
  36.0 9.6 %conditional.3 = (f32[80,2048]{1,0:T(8,128)S(1)}, f32[2048]{0:T(1024)}, f32[2048]{0:T(1024)}, f32[10,80]{1,0:T(8,128)S(1)}, f32[2048]{0:T(1024)}) conditional(s32[]{:T(128)} %convert_element_type.175, () %tuple.366, (s32[]{:T(128)}, f32[10,2048]{1,0:T(8,128)}, f32[10,80]{1,0:T(8,128)}, f32[4,80]{1,0:T(4,128)}, f32[80,2048]{1,0:T(8,128)}, ...), branch_computations={%region_1.1_spmd, %region_2.83_spmd} | conditional | flops 15945717760 | bytes 379194208 | solution.py:181
  52.2 10.3 %collective-permute-done.1 = f32[2048]{0:T(1024)S(1)} collective-permute-done((f32[2048]{0:T(1024)}, f32[2048]{0:T(1024)S(1)}, u32[]{:S(2)}, u32[]{:S(2)}) %collective-permute-start.1) | collective-permute-done | bytes 8224 | tf_op jit(solution)/shard_map/while/body/eval_jaxpr/ppermute | solution.py:16
  72.8 8.7 %collective-permute-done.1 = f32[2048]{0:T(1024)S(1)} collective-permute-done((f32[2048]{0:T(1024)}, f32[2048]{0:T(1024)S(1)}, u32[]{:S(2)}, u32[]{:S(2)}) %collective-permute-start.1) | collective-permute-done | bytes 8224 | tf_op jit(solution)/shard_map/while/body/eval_jaxpr/ppermute | solution.py:16
  91.7 472.9 %collective-permute-done.1 = f32[2048]{0:T(1024)S(1)} collective-permute-done((f32[2048]{0:T(1024)}, f32[2048]{0:T(1024)S(1)}, u32[]{:S(2)}, u32[]{:S(2)}) %collective-permute-start.1) | collective-permute-done | bytes 8224 | tf_op jit(solution)/shard_map/while/body/eval_jaxpr/ppermute | solution.py:16
  565.5 159.6 %conditional.3 = (f32[80,2048]{1,0:T(8,128)S(1)}, f32[2048]{0:T(1024)}, f32[2048]{0:T(1024)}, f32[10,80]{1,0:T(8,128)S(1)}, f32[2048]{0:T(1024)}) conditional(s32[]{:T(128)} %convert_element_type.175, () %tuple.366, (s32[]{:T(128)}, f32[10,2048]{1,0:T(8,128)}, f32[10,80]{1,0:T(8,128)}, f32[4,80]{1,0:T(4,128)}, f32[80,2048]{1,0:T(8,128)}, ...), branch_computations={%region_1.1_spmd, %region_2.83_spmd} | conditional | flops 15945717760 | bytes 379194208 | solution.py:181
  571.0 3.7 multiply_reduce_fusion.29
  579.8 3.0 multiply_reduce_fusion.28
  585.3 3.0 multiply_reduce_fusion.27
  591.2 3.1 multiply_reduce_fusion.26
  597.6 3.0 multiply_reduce_fusion.25
  603.3 3.3 multiply_reduce_fusion.24
  609.8 3.2 multiply_reduce_fusion.23
  616.5 3.3 multiply_reduce_fusion.22
  623.0 3.1 multiply_reduce_fusion.21
  711.4 2.5 multiply_reduce_fusion.1
  716.1 2.6 multiply_reduce_fusion
  732.5 7.9 %collective-permute-done.1 = f32[2048]{0:T(1024)S(1)} collective-permute-done((f32[2048]{0:T(1024)}, f32[2048]{0:T(1024)S(1)}, u32[]{:S(2)}, u32[]{:S(2)}) %collective-permute-start.1) | collective-permute-done | bytes 8224 | tf_op jit(solution)/shard_map/while/body/eval_jaxpr/ppermute | solution.py:16
  742.4 12.8 %psum.14 = f32[10,80]{1,0:T(8,128)} all-reduce(f32[10,80]{1,0:T(8,128)} %get-tuple-element.303), channel_id=1, replica_groups=mesh['tm'=4,'paths'=8] {'paths'}, use_global_device_ids=true, to_apply=%region_85.86 | all-reduce | flops 800 | bytes 6400 | tf_op jit(solution)/shard_map/psum | solution.py:190
  755.2 9.2 %psum.15 = f32[2048]{0:T(1024)} all-reduce(f32[2048]{0:T(1024)} %get-tuple-element.304), channel_id=1, replica_groups=mesh['tm'=4,'paths'=8] {'tm'}, use_global_device_ids=true, to_apply=%region_86.87 | all-reduce | flops 2048 | bytes 16384 | tf_op jit(solution)/shard_map/psum | solution.py:118
  (681 shorter events, 170.3 us)
Async XLA Ops:
  0.6 31.6 %collective-permute-start.3 = (f32[80,2048]{1,0:T(8,128)}, f32[80,2048]{1,0:T(8,128)S(1)}, u32[]{:S(2)}, u32[]{:S(2)}) collective-permute-start(f32[80,2048]{1,0:T(8,128)} %bitcast.999), channel_id=1, source_target_pairs={{0,8},{8,16},{16,24},{1,9},{9,17},{17,25},{2,10},{10,18},{18,26},{... | collective-permute-start | bytes 1966088 | tf_op jit(solution)/shard_map/ppermute | solution.py:16
  5.6 25.4 %collective-permute-start.4 = (f32[2048]{0:T(1024)}, f32[2048]{0:T(1024)S(1)}, u32[]{:S(2)}, u32[]{:S(2)}) collective-permute-start(f32[2048]{0:T(1024)} %bitcast.1000), channel_id=1, source_target_pairs={{0,8},{8,16},{16,24},{1,9},{9,17},{17,25},{2,10},{10,18},{18,26},{... | collective-permute-start | bytes 24584 | tf_op jit(solution)/shard_map/ppermute | solution.py:16
  9.1 22.6 %collective-permute-start.5 = (f32[2048]{0:T(1024)}, f32[2048]{0:T(1024)S(1)}, u32[]{:S(2)}, u32[]{:S(2)}) collective-permute-start(f32[2048]{0:T(1024)} %bitcast.1001), channel_id=1, source_target_pairs={{0,8},{8,16},{16,24},{1,9},{9,17},{17,25},{2,10},{10,18},{18,26},{... | collective-permute-start | bytes 24584 | tf_op jit(solution)/shard_map/ppermute | solution.py:16
  46.4 16.2 %collective-permute-start = (f32[80,2048]{1,0:T(8,128)}, f32[80,2048]{1,0:T(8,128)S(1)}, u32[]{:S(2)}, u32[]{:S(2)}) collective-permute-start(f32[80,2048]{1,0:T(8,128)} %copy-done.37), channel_id=1, source_target_pairs={{8,0},{16,8},{24,16},{9,1},{17,9},{25,17},{10,2},{18,10},{26,18},{... | collective-permute-start | bytes 1966088 | tf_op jit(solution)/shard_map/while/body/eval_jaxpr/ppermute | solution.py:16
  47.7 14.8 %collective-permute-start.1 = (f32[2048]{0:T(1024)}, f32[2048]{0:T(1024)S(1)}, u32[]{:S(2)}, u32[]{:S(2)}) collective-permute-start(f32[2048]{0:T(1024)} %get-tuple-element.968), channel_id=1, source_target_pairs={{8,0},{16,8},{24,16},{9,1},{17,9},{25,17},{10,2},{18,10},{26,18},{... | collective-permute-start | bytes 24584 | tf_op jit(solution)/shard_map/while/body/eval_jaxpr/ppermute | solution.py:16
  49.0 13.6 %collective-permute-start.2 = (f32[2048]{0:T(1024)}, f32[2048]{0:T(1024)S(1)}, u32[]{:S(2)}, u32[]{:S(2)}) collective-permute-start(f32[2048]{0:T(1024)} %get-tuple-element.969), channel_id=1, source_target_pairs={{8,0},{16,8},{24,16},{9,1},{17,9},{25,17},{10,2},{18,10},{26,18},{... | collective-permute-start | bytes 24584 | tf_op jit(solution)/shard_map/while/body/eval_jaxpr/ppermute | solution.py:16
  66.3 15.3 %collective-permute-start = (f32[80,2048]{1,0:T(8,128)}, f32[80,2048]{1,0:T(8,128)S(1)}, u32[]{:S(2)}, u32[]{:S(2)}) collective-permute-start(f32[80,2048]{1,0:T(8,128)} %copy-done.37), channel_id=1, source_target_pairs={{8,0},{16,8},{24,16},{9,1},{17,9},{25,17},{10,2},{18,10},{26,18},{... | collective-permute-start | bytes 1966088 | tf_op jit(solution)/shard_map/while/body/eval_jaxpr/ppermute | solution.py:16
  67.6 13.9 %collective-permute-start.1 = (f32[2048]{0:T(1024)}, f32[2048]{0:T(1024)S(1)}, u32[]{:S(2)}, u32[]{:S(2)}) collective-permute-start(f32[2048]{0:T(1024)} %get-tuple-element.968), channel_id=1, source_target_pairs={{8,0},{16,8},{24,16},{9,1},{17,9},{25,17},{10,2},{18,10},{26,18},{... | collective-permute-start | bytes 24584 | tf_op jit(solution)/shard_map/while/body/eval_jaxpr/ppermute | solution.py:16
  68.9 12.7 %collective-permute-start.2 = (f32[2048]{0:T(1024)}, f32[2048]{0:T(1024)S(1)}, u32[]{:S(2)}, u32[]{:S(2)}) collective-permute-start(f32[2048]{0:T(1024)} %get-tuple-element.969), channel_id=1, source_target_pairs={{8,0},{16,8},{24,16},{9,1},{17,9},{25,17},{10,2},{18,10},{26,18},{... | collective-permute-start | bytes 24584 | tf_op jit(solution)/shard_map/while/body/eval_jaxpr/ppermute | solution.py:16
  85.2 479.5 %collective-permute-start = (f32[80,2048]{1,0:T(8,128)}, f32[80,2048]{1,0:T(8,128)S(1)}, u32[]{:S(2)}, u32[]{:S(2)}) collective-permute-start(f32[80,2048]{1,0:T(8,128)} %copy-done.37), channel_id=1, source_target_pairs={{8,0},{16,8},{24,16},{9,1},{17,9},{25,17},{10,2},{18,10},{26,18},{... | collective-permute-start | bytes 1966088 | tf_op jit(solution)/shard_map/while/body/eval_jaxpr/ppermute | solution.py:16
  86.5 478.1 %collective-permute-start.1 = (f32[2048]{0:T(1024)}, f32[2048]{0:T(1024)S(1)}, u32[]{:S(2)}, u32[]{:S(2)}) collective-permute-start(f32[2048]{0:T(1024)} %get-tuple-element.968), channel_id=1, source_target_pairs={{8,0},{16,8},{24,16},{9,1},{17,9},{25,17},{10,2},{18,10},{26,18},{... | collective-permute-start | bytes 24584 | tf_op jit(solution)/shard_map/while/body/eval_jaxpr/ppermute | solution.py:16
  87.8 476.9 %collective-permute-start.2 = (f32[2048]{0:T(1024)}, f32[2048]{0:T(1024)S(1)}, u32[]{:S(2)}, u32[]{:S(2)}) collective-permute-start(f32[2048]{0:T(1024)} %get-tuple-element.969), channel_id=1, source_target_pairs={{8,0},{16,8},{24,16},{9,1},{17,9},{25,17},{10,2},{18,10},{26,18},{... | collective-permute-start | bytes 24584 | tf_op jit(solution)/shard_map/while/body/eval_jaxpr/ppermute | solution.py:16
  566.4 24.7 %copy-start.114 = (f32[80]{0:T(128)}, f32[80]{0:T(128)S(1)}, u32[]{:S(2)}) copy-start(f32[80]{0:T(128)S(1)} %get-tuple-element.632) | copy-start | bytes 964 | tf_op jit(solution)/shard_map/while/body/eval_jaxpr/cond
  577.0 46.0 %copy-start.196 = (f32[80]{0:T(128)}, f32[80]{0:T(128)S(1)}, u32[]{:S(2)}) copy-start(f32[80]{0:T(128)S(1)} %and_convert_fusion) | copy-start | bytes 964 | tf_op jit(solution)/shard_map/while/body/eval_jaxpr/cond
  577.0 39.4 %copy-start.194 = (f32[80]{0:T(128)}, f32[80]{0:T(128)S(1)}, u32[]{:S(2)}) copy-start(f32[80]{0:T(128)S(1)} %and_convert_fusion.1) | copy-start | bytes 964 | tf_op jit(solution)/shard_map/while/body/eval_jaxpr/cond
  577.0 32.7 %copy-start.192 = (f32[80]{0:T(128)}, f32[80]{0:T(128)S(1)}, u32[]{:S(2)}) copy-start(f32[80]{0:T(128)S(1)} %and_convert_fusion.2) | copy-start | bytes 964 | tf_op jit(solution)/shard_map/while/body/eval_jaxpr/cond
  577.1 26.2 %copy-start.190 = (f32[80]{0:T(128)}, f32[80]{0:T(128)S(1)}, u32[]{:S(2)}) copy-start(f32[80]{0:T(128)S(1)} %and_convert_fusion.3) | copy-start | bytes 964 | tf_op jit(solution)/shard_map/while/body/eval_jaxpr/cond
  577.1 20.4 %copy-start.188 = (f32[80]{0:T(128)}, f32[80]{0:T(128)S(1)}, u32[]{:S(2)}) copy-start(f32[80]{0:T(128)S(1)} %and_convert_fusion.4) | copy-start | bytes 964 | tf_op jit(solution)/shard_map/while/body/eval_jaxpr/cond
  595.1 21.3 %copy-start.122 = (f32[80]{0:T(128)}, f32[80]{0:T(128)S(1)}, u32[]{:S(2)}) copy-start(f32[80]{0:T(128)S(1)} %get-tuple-element.782) | copy-start | bytes 964 | tf_op jit(solution)/shard_map/while/body/eval_jaxpr/cond
  595.1 27.8 %copy-start.124 = (f32[80]{0:T(128)}, f32[80]{0:T(128)S(1)}, u32[]{:S(2)}) copy-start(f32[80]{0:T(128)S(1)} %get-tuple-element.780) | copy-start | bytes 964 | tf_op jit(solution)/shard_map/while/body/eval_jaxpr/cond
  595.1 34.1 %copy-start.126 = (f32[80]{0:T(128)}, f32[80]{0:T(128)S(1)}, u32[]{:S(2)}) copy-start(f32[80]{0:T(128)S(1)} %get-tuple-element.620) | copy-start | bytes 964 | tf_op jit(solution)/shard_map/while/body/eval_jaxpr/cond
  726.0 14.5 %collective-permute-start = (f32[80,2048]{1,0:T(8,128)}, f32[80,2048]{1,0:T(8,128)S(1)}, u32[]{:S(2)}, u32[]{:S(2)}) collective-permute-start(f32[80,2048]{1,0:T(8,128)} %copy-done.37), channel_id=1, source_target_pairs={{8,0},{16,8},{24,16},{9,1},{17,9},{25,17},{10,2},{18,10},{26,18},{... | collective-permute-start | bytes 1966088 | tf_op jit(solution)/shard_map/while/body/eval_jaxpr/ppermute | solution.py:16
  727.3 13.1 %collective-permute-start.1 = (f32[2048]{0:T(1024)}, f32[2048]{0:T(1024)S(1)}, u32[]{:S(2)}, u32[]{:S(2)}) collective-permute-start(f32[2048]{0:T(1024)} %get-tuple-element.968), channel_id=1, source_target_pairs={{8,0},{16,8},{24,16},{9,1},{17,9},{25,17},{10,2},{18,10},{26,18},{... | collective-permute-start | bytes 24584 | tf_op jit(solution)/shard_map/while/body/eval_jaxpr/ppermute | solution.py:16
  728.6 11.9 %collective-permute-start.2 = (f32[2048]{0:T(1024)}, f32[2048]{0:T(1024)S(1)}, u32[]{:S(2)}, u32[]{:S(2)}) collective-permute-start(f32[2048]{0:T(1024)} %get-tuple-element.969), channel_id=1, source_target_pairs={{8,0},{16,8},{24,16},{9,1},{17,9},{25,17},{10,2},{18,10},{26,18},{... | collective-permute-start | bytes 24584 | tf_op jit(solution)/shard_map/while/body/eval_jaxpr/ppermute | solution.py:16
  (201 other events, 411.9 us)
where the time goes:
time: 769 us; the launch traced here: 765 us
  waiting for transfers between devices  500 us (65%)
  matrix products  103 us (13%)
  other arithmetic  46.5 us (6%)
  blocking collectives  37.9 us (5%)
  local copies, waits for them, and re-layouts  34.9 us (5%)
  starting transfers between devices  27.4 us (4%)
  loops' own time  13.7 us (2%)
    ppermute x15, waiting for transfers between devices, passed_along(): lax.ppermute(value, axis, [(source, source + steps) for source in range(i...  500 us
    dot_general x20, matrix products, segment(): jnp.einsum('ij,fjp->fip', triangle, factor_loads[:, :, None] * scaled[Non...  37.6 us
    dot_general x10, matrix products, segment(): jnp.einsum('fi,fp->ip', factor_loads, shock_rows[offset_date], precision=...  31.2 us
    ppermute x15, starting transfers between devices, passed_along(): lax.ppermute(value, axis, [(source, source + steps) for source in range(i...  27.4 us
    dot_general x20, matrix products, segment(): jnp.dot(triangle, living[:, None] * jnp.log1p(ACCRUAL * current), precisi...  26.9 us
    all_gather x1, blocking collectives, local(): table = lax.all_gather(regress, 'tm', axis=0, tiled=True)  16 us
  transfers between devices with their start and end apart: 15, of which 8 were waited for; matrix products, arithmetic and copies ran while one was open for 2% of the time, Pallas kernels for 0%

commit v1 on v0

v1 whole, which is shorter than its diff:
```python
import functools

import jax
import jax.numpy as jnp
from jax import lax
from jax.experimental import pallas as pl
from jax.experimental.pallas import tpu as pltpu
from jax.sharding import PartitionSpec as P

ACCRUAL = 0.25
STRIKE = 0.04
SMOOTHING = 0.01
NOTIONAL = 100.0
LANES = 128
BLOCK = 8


def kernel(
    place_ref,
    vol_ref,
    ratio_ref,
    regress_ref,
    slot_ref,
    curve_ref,
    *refs,
    shards,
    per_shard,
    forwards,
    factors,
    basis,
    low_row,
):
    block_refs = refs[:shards]
    vega_ref, value_ref = refs[shards : shards + 2]
    (
        inbox,
        rate,
        disc,
        res_growth,
        res_exp,
        res_slope,
        res_tilt,
        res_drive,
        res_disc,
        res_sum,
        grads,
        annuities,
        finals,
        numers,
        fixes,
        seeds_a,
        seeds_b,
        numer_adj,
        survs,
        chances,
        pays,
        adjoint,
        arrived,
    ) = refs[shards + 2 :]
    dates = shards * per_shard
    blocks = forwards // BLOCK
    sub = value_ref.shape[0]
    tile = (sub, LANES)
    place = place_ref[0]
    row_flag = per_shard * factors
    row_rates = row_flag + per_shard
    row_numer = row_rates + forwards - low_row
    row_survive = row_numer + 1

    def fetch(step):
        source = lax.rem(place - step + shards, shards)
        return pltpu.make_async_copy(block_refs[step], inbox.at[source], arrived.at[step])

    for step in range(shards):
        fetch(step).start()
    for step in range(shards):
        fetch(step).wait()

    def first_block(opening):
        return opening // BLOCK

    def forward_date(shard, offset, carry):
        pos, numer = carry
        date = shard * per_shard + offset
        opening = 2 * date + 1
        is_start = date == 0
        horizon = jnp.where(is_start, ACCRUAL, 2.0 * ACCRUAL)
        inv_root = jnp.where(is_start, ACCRUAL**-0.5, (2.0 * ACCRUAL) ** -0.5)
        near = jnp.maximum(opening - 2, 0)
        last = opening - 1
        numer = numer * (1.0 + rate[last])
        numer = numer * jnp.where(is_start, 1.0, 1.0 + rate[near])
        numers[date] = numer
        fixes[2 * date] = disc[near]
        fixes[2 * date + 1] = disc[last]
        sums = tuple(inbox[shard, offset * factors + f] * inv_root for f in range(factors))

        def one_block(block, state, masked):
            pos, sums, bond, total = state
            sums = list(sums)
            for inner in range(BLOCK):
                row = block * BLOCK + inner
                at = pos * BLOCK + inner
                vol = vol_ref[date * forwards + row]
                if masked:
                    alive = row >= opening
                    vol = jnp.where(alive, vol, 0.0)
                lead = vol * ratio_ref[row]
                half = vol * ratio_ref[forwards + row]
                timed = horizon * lead
                old = disc[row]
                drive = lead * (1.0 - old)
                sums[0] = sums[0] + drive
                tilt = sums[0]
                for f in range(1, factors):
                    scale = ratio_ref[(f + 1) * forwards + row]
                    sums[f] = sums[f] + scale * drive
                    tilt = tilt + scale * sums[f]
                tilt = tilt - half
                grow = jnp.exp(timed * tilt)
                new = rate[row] * grow
                fresh = 1.0 / (1.0 + new)
                rate[row] = new
                disc[row] = fresh
                res_growth[at] = timed * new
                res_exp[at] = grow
                res_slope[at] = lead * (old * old)
                res_tilt[at] = tilt - half
                res_drive[at] = drive
                res_sum[at] = total
                if masked:
                    mask = alive.astype(jnp.float32)
                    res_disc[at] = fresh * mask
                    bond = bond * jnp.where(alive, fresh, 1.0)
                    total = total + bond * mask
                else:
                    res_disc[at] = fresh
                    bond = bond * fresh
                    total = total + bond
            return (pos + 1, tuple(sums), bond, total)

        begin = first_block(opening)
        state = one_block(
            begin, (pos, sums, jnp.ones(tile, jnp.float32), jnp.zeros(tile, jnp.float32)), True
        )
        pos, _, bond, total = lax.fori_loop(
            begin + 1, blocks, lambda block, s: one_block(block, s, False), state
        )
        annuities[date] = ACCRUAL * total
        finals[date] = bond
        return (pos, numer)

    pos = jnp.int32(0)
    ends = []
    for shard in range(shards):
        if shard == 0:
            def fill(row, _):
                start = jnp.full(tile, ACCRUAL * curve_ref[row], jnp.float32)
                rate[row] = start
                disc[row] = 1.0 / (1.0 + start)
                return 0

            lax.fori_loop(0, forwards, fill, 0, unroll=BLOCK)
            numer = jnp.ones(tile, jnp.float32)
        else:
            lowest = (2 * shard * per_shard - 1) // BLOCK * BLOCK

            def fill(row, _, shard=shard):
                start = ACCRUAL * inbox[shard - 1, row_rates + row - low_row]
                rate[row] = start
                disc[row] = 1.0 / (1.0 + start)
                return 0

            lax.fori_loop(lowest, forwards, fill, 0, unroll=BLOCK)
            numer = inbox[shard - 1, row_numer]
        pos, numer = lax.fori_loop(
            0, per_shard, functools.partial(forward_date, shard), (pos, numer)
        )
        ends.append(numer)

    value = jnp.zeros(tile, jnp.float32)
    for shard in range(shards):
        if shard == 0:
            survive = jnp.ones(tile, jnp.float32)
        else:
            survive = inbox[shard - 1, row_survive]

        def stage(offset, carry, shard=shard):
            survive, value = carry
            date = shard * per_shard + offset
            annuity = annuities[date]
            floating = 1.0 - finals[date]
            slot = slot_ref[date] * basis
            w = [regress_ref[slot + q] for q in range(basis)]
            inverse = 1.0 / annuity
            swap = floating * inverse
            money = (swap - STRIKE) * (1.0 / SMOOTHING)
            exercise = floating - STRIKE * annuity
            inner = w[3] + money * (w[4] + money * w[5])
            continuation = w[0] + money * (w[1] + money * w[2]) + annuity * inner
            sigmoid = jax.nn.sigmoid((exercise - continuation) * (1.0 / SMOOTHING))
            flag = inbox[shard, row_flag + offset]
            chance = flag * sigmoid
            pay = NOTIONAL * exercise / numers[date]
            slope = chance * (1.0 - sigmoid) * (1.0 / SMOOTHING)
            money_adj = (
                w[1] + 2.0 * (w[2] * money) + annuity * (w[4] + 2.0 * (w[5] * money))
            ) * (1.0 / SMOOTHING)
            tilt_money = money_adj * inverse
            seeds_a[2 * date] = slope * (-STRIKE - inner + tilt_money * swap)
            seeds_a[2 * date + 1] = slope * (1.0 - tilt_money)
            chances[date] = chance
            pays[date] = pay
            survs[date] = survive
            value = value + survive * chance * pay
            return (survive * (1.0 - chance), value)

        survive, value = lax.fori_loop(0, per_shard, stage, (survive, value), unroll=5)
    value_ref[...] = value

    gain_adj = jnp.zeros(tile, jnp.float32)
    log_adj = jnp.zeros(tile, jnp.float32)
    for shard in reversed(range(shards)):

        def unwind(step, carry, shard=shard):
            late, log_adj = carry
            date = shard * per_shard + per_shard - 1 - step
            chance = chances[date]
            pay = pays[date]
            survive = survs[date]
            chance_adj = survive * (pay - late)
            direct = (NOTIONAL * survive) * chance / numers[date]
            annuity_adj = chance_adj * seeds_a[2 * date] - STRIKE * direct
            float_adj = chance_adj * seeds_a[2 * date + 1] + direct
            seeds_b[2 * date] = annuity_adj * annuities[date] - float_adj * finals[date]
            seeds_b[2 * date + 1] = ACCRUAL * annuity_adj
            gain = chance * pay
            log_adj = log_adj - survive * gain
            numer_adj[date] = log_adj
            return (gain + late * (1.0 - chance), log_adj)

        gain_adj, log_adj = lax.fori_loop(0, per_shard, unwind, (gain_adj, log_adj), unroll=5)
        if shard > 0:
            log_adj = log_adj * ends[shard - 1] / inbox[shard - 1, row_numer]

    def clear(row, _):
        adjoint[row] = jnp.zeros(tile, jnp.float32)
        return 0

    lax.fori_loop(0, forwards, clear, 0, unroll=BLOCK)

    def backward_date(step, pos):
        date = dates - 1 - step
        opening = 2 * date + 1
        seed_level = seeds_b[2 * date]
        seed_slope = seeds_b[2 * date + 1]

        def one_block(back, state):
            pos, sums = state
            sums = list(sums)
            block = blocks - 1 - back
            pos = pos - 1
            for inner in reversed(range(BLOCK)):
                row = block * BLOCK + inner
                at = pos * BLOCK + inner
                pull = (seed_level - seed_slope * res_sum[at]) * res_disc[at]
                inward = adjoint[row] - pull
                timed = inward * res_growth[at]
                sums[0] = sums[0] + timed
                drive_adj = sums[0]
                for f in range(1, factors):
                    scale = ratio_ref[(f + 1) * forwards + row]
                    sums[f] = sums[f] + scale * timed
                    drive_adj = drive_adj + scale * sums[f]
                adjoint[row] = inward * res_exp[at] + drive_adj * res_slope[at]
                grads[date * forwards + row] = timed * res_tilt[at] + drive_adj * res_drive[at]
            return (pos, tuple(sums))

        zero = jnp.zeros(tile, jnp.float32)
        pos, _ = lax.fori_loop(
            0, blocks - first_block(opening), one_block, (pos, (zero,) * factors)
        )
        near = jnp.maximum(opening - 2, 0)
        last = opening - 1
        level = numer_adj[date]
        adjoint[near] = level * fixes[2 * date]
        adjoint[last] = level * fixes[2 * date + 1]
        return pos

    lax.fori_loop(0, dates, backward_date, pos)

    ones = jnp.ones((BLOCK, LANES), jnp.float32)

    def collect(date, _):
        picked = grads[pl.ds(date * forwards, forwards)]
        summed = jnp.sum(picked, axis=1)
        row = lax.dot_general(
            ones, summed, (((1,), (1,)), ((), ())),
            precision=lax.Precision.HIGHEST, preferred_element_type=jnp.float32,
        )
        vega_ref[date] = row[0:1]
        return 0

    lax.fori_loop(0, dates, collect, 0)


def turned(parts, start):
    doubled = jnp.concatenate(parts + parts, axis=0)
    return lax.dynamic_slice_in_dim(doubled, start * parts[0].shape[0], len(parts) * parts[0].shape[0], 0)


def by_source(own, received, place):
    count = len(received) + 1
    return turned([own] + received[::-1], lax.rem(count - place, count))


def exchange(blocks, axis, place):
    count = lax.axis_size(axis)
    own = lax.dynamic_index_in_dim(blocks, place, 0, keepdims=False)
    received = []
    for step in range(1, count):
        sent = lax.dynamic_index_in_dim(blocks, lax.rem(place + step, count), 0, keepdims=False)
        received.append(
            lax.ppermute(sent, axis, [(s, (s + step) % count) for s in range(count)])
        )
    return own, received


def total_over(value, axis):
    count = lax.axis_size(axis)
    if count & (count - 1):
        return lax.psum(value, axis)
    step = 1
    while step < count:
        value = value + lax.ppermute(value, axis, [(s, s ^ step) for s in range(count)])
        step *= 2
    return value


def local(
    start_curve,
    loadings,
    vols,
    shocks,
    exercise_bits,
    regress,
    date_slot,
    ck_rates,
    ck_numer,
    ck_survive,
):
    shards = lax.axis_size("tm")
    groups = lax.axis_size("paths")
    place = lax.axis_index("tm")
    per_shard, forwards = vols.shape
    factors, paths = shocks.shape[1:]
    basis = regress.shape[1]
    dates = shards * per_shard
    per_device = paths // shards
    sub = per_device // LANES
    unit = sub * LANES
    low_row = max(0, (2 * per_shard - 1) // BLOCK * BLOCK)

    def blocked(rows):
        return rows.reshape(-1, shards, sub, LANES).transpose(1, 0, 2, 3)

    small = jnp.concatenate(
        [vols.reshape(-1), regress.reshape(-1), date_slot.astype(jnp.float32)]
    )
    small_rows = -(-small.shape[0] // unit)
    small = jnp.pad(small, (0, small_rows * unit - small.shape[0]))
    payload = jnp.concatenate(
        [
            blocked(shocks.reshape(per_shard * factors, paths)),
            blocked(exercise_bits.astype(jnp.float32)),
            blocked(ck_rates[0, low_row:]),
            blocked(ck_numer),
            blocked(ck_survive),
            jnp.broadcast_to(small.reshape(1, small_rows, sub, LANES), (shards, small_rows, sub, LANES)),
        ],
        axis=1,
    )
    rows = payload.shape[1]
    own, received = exchange(payload, "tm", place)
    smalls = by_source(
        own[rows - small_rows :].reshape(1, -1),
        [part[rows - small_rows :].reshape(1, -1) for part in received],
        place,
    )
    cut = per_shard * forwards
    vol_all = smalls[:, :cut].reshape(-1)
    regress_all = smalls[:, cut : cut + per_shard * basis].reshape(-1)
    slot_all = (
        smalls[:, cut + per_shard * basis : cut + per_shard * (basis + 1)]
        .reshape(-1)
        .astype(jnp.int32)
    )
    loads = loadings / jnp.sqrt(jnp.sum(loadings * loadings, axis=0, keepdims=True))
    ratios = jnp.concatenate([loads[0], 0.5 / loads[0], (loads[1:] / loads[:1]).reshape(-1)])

    triangle = sum(
        forwards // BLOCK - min((2 * d + 1) // BLOCK, forwards // BLOCK - 1) for d in range(dates)
    )
    tile = (sub, LANES)
    f32 = jnp.float32
    residual = pltpu.VMEM((triangle * BLOCK,) + tile, f32)
    per_date = pltpu.VMEM((dates,) + tile, f32)
    two_per_date = pltpu.VMEM((2 * dates,) + tile, f32)
    per_forward = pltpu.VMEM((forwards,) + tile, f32)
    smem = pl.BlockSpec(memory_space=pltpu.SMEM)
    vega_part, value_part = pl.pallas_call(
        functools.partial(
            kernel,
            shards=shards,
            per_shard=per_shard,
            forwards=forwards,
            factors=factors,
            basis=basis,
            low_row=low_row,
        ),
        out_shape=(
            jax.ShapeDtypeStruct((dates, 1, forwards), f32),
            jax.ShapeDtypeStruct(tile, f32),
        ),
        in_specs=[smem] * 6 + [pl.BlockSpec(memory_space=pl.ANY)] * shards,
        out_specs=(
            pl.BlockSpec(memory_space=pltpu.VMEM),
            pl.BlockSpec(memory_space=pltpu.VMEM),
        ),
        scratch_shapes=[
            pltpu.VMEM((shards, rows) + tile, f32),
            per_forward,
            per_forward,
            residual,
            residual,
            residual,
            residual,
            residual,
            residual,
            residual,
            pltpu.VMEM((dates * forwards,) + tile, f32),
            per_date,
            per_date,
            per_date,
            two_per_date,
            two_per_date,
            two_per_date,
            per_date,
            per_date,
            per_date,
            per_date,
            per_forward,
            pltpu.SemaphoreType.DMA((shards,)),
        ],
        compiler_params=pltpu.CompilerParams(vmem_limit_bytes=56 * 1024 * 1024),
        name="sweep",
    )(
        place.reshape(1).astype(jnp.int32),
        vol_all,
        ratios,
        regress_all,
        slot_all,
        start_curve,
        own,
        *received,
    )

    parts = vega_part.reshape(shards, cut)
    tail = value_part.reshape(1, per_device)
    message = jnp.concatenate([parts, jnp.broadcast_to(tail, (shards, per_device))], axis=1)
    mine, others = exchange(message, "tm", place)
    path_value = by_source(
        mine[cut:].reshape(1, -1), [part[cut:].reshape(1, -1) for part in others], place
    ).reshape(-1)
    summed = mine[:cut]
    for part in others:
        summed = summed + part[:cut]
    summed = total_over(summed.reshape(per_shard, forwards), "paths")
    date = place * per_shard + jnp.arange(per_shard, dtype=jnp.int32)
    alive = jnp.arange(forwards, dtype=jnp.int32)[None, :] >= 2 * date[:, None] + 1
    weight = NOTIONAL / (paths * groups)
    vega = jnp.where(alive, summed * (weight / vols), 0.0)
    return (vega, path_value)


def solution(mesh):
    return jax.shard_map(
        local,
        mesh=mesh,
        in_specs=(
            P(),
            P(),
            P("tm", None),
            P("tm", None, "paths"),
            P("tm", "paths"),
            P("tm", None),
            P("tm"),
            P("tm", None, "paths"),
            P("tm", "paths"),
            P("tm", "paths"),
        ),
        out_specs=(P("tm", None), P("paths")),
        check_vma=False,
    )
```

time: 769 us -> 94 us (0.12)
  waiting for transfers between devices: 500 us -> 26.4 us
  matrix products: 103 us -> 0 us
  other arithmetic: 46.5 us -> 2.99 us
  blocking collectives: 37.9 us -> 0 us
  Pallas kernels: 0 us -> 37.4 us
  local copies, waits for them, and re-layouts: 34.9 us -> 11.8 us
  loops' own time: 13.7 us -> 0 us
  starting transfers between devices: 27.4 us -> 14 us
    ppermute x15 -> x9, waiting for transfers between devices: 500 us -> 26.4 us  [the longest x6 21.9 us: exchange(): lax.ppermute(sent, axis, [(s, (s + step) % count) for s in range(count)])]
    dot_general x61 -> x0, matrix products: 103 us -> none  [the longest x20 37.6 us: segment(): jnp.einsum('ij,fjp->fip', triangle, factor_loads[:, :, None] * scaled[Non...]
    pallas_call x0 -> x1, Pallas kernels: none -> 37.4 us  [local(): pl.pallas_call(functools.partial(kernel, shards=shards, per_shard=per_sha...]
    psum x2 -> x0, blocking collectives: 22 us -> none  [the longest x1 12.8 us: local(): vega = lax.psum(vega_part, 'paths')]
    mul x62 -> x0, other arithmetic: 16.1 us -> none  [the longest x10 6.35 us: segment(): annuity * moneyness * moneyness]
    all_gather x1 -> x0, blocking collectives: 16 us -> none  [local(): table = lax.all_gather(regress, 'tm', axis=0, tiled=True)]
    another operation x5 -> x0, loops' own time: 13.7 us -> none  [the longest x4 12.2 us: take_turn(): lax.cond(active, do_pullback, do_nothing, incoming)]
    ppermute x15 -> x9, starting transfers between devices: 27.4 us -> 14 us  [the longest x6 10.9 us: exchange(): lax.ppermute(sent, axis, [(s, (s + step) % count) for s in range(count)])]
  transfers between devices with their start and end apart: 15 -> 9, of which waited for: 8 -> 6; matrix products, arithmetic and copies ran while one was open for 2% -> 2% of each run, Pallas kernels for 0% -> 0%
where the time goes in v1:
time: 94 us; the launch traced here: 93.5 us
  Pallas kernels  37.4 us (40%)
  waiting for transfers between devices  26.4 us (28%)
  starting transfers between devices  14 us (15%)
  local copies, waits for them, and re-layouts  11.8 us (13%)
  other arithmetic  2.99 us (3%)
    pallas_call x1, Pallas kernels, local(): pl.pallas_call(functools.partial(kernel, shards=shards, per_shard=per_sha...  37.4 us
    ppermute x6, waiting for transfers between devices, exchange(): lax.ppermute(sent, axis, [(s, (s + step) % count) for s in range(count)])  21.9 us
    ppermute x6, starting transfers between devices, exchange(): lax.ppermute(sent, axis, [(s, (s + step) % count) for s in range(count)])  10.9 us
    unnamed x30, local copies, waits for them, and re-layouts  4.56 us
    ppermute x3, waiting for transfers between devices, total_over(): lax.ppermute(value, axis, [(s, s ^ step) for s in range(count)])  4.5 us
    ppermute x3, starting transfers between devices, total_over(): lax.ppermute(value, axis, [(s, s ^ step) for s in range(count)])  3.08 us
  transfers between devices with their start and end apart: 9, of which 6 were waited for; matrix products, arithmetic and copies ran while one was open for 2% of the time, Pallas kernels for 0%

profile of v1, /device:TPU:0, one launch (start us, length us, event | category | flops | bytes accessed | tf_op | source)
XLA Modules:
  0.0 93.5 jit_solution(6689330226939693430)
XLA Ops:
  0.6 1.2 %reshape_reshape.3 = f32[40,4,4,128]{3,2,1,0:T(4,128)S(1)} reshape(f32[10,4,2048]{2,1,0:T(4,128)} %param.13) | data formatting | bytes 655360 | tf_op jit(solution)/shard_map/reshape;reshape | solution.py:365
  2.0 0.8 copy-done.3
  2.9 1.0 %slice-done = f32[1,64,2048]{2,1,0:T(8,128)S(1)} async-done(((f32[1,80,2048]{2,1,0:T(8,128)}), f32[1,64,2048]{2,1,0:T(8,128)S(1)}, s32[]{:S(2)}) %slice-start) | async-done | bytes 524312 | tf_op jit(solution)/shard_map/slice | solution.py:376
  6.1 0.7 copy-done.7
  6.9 0.8 dynamic-slice_bitcast_fusion.3
  7.7 5.1 %collective-permute-start = (f32[118,4,128]{2,1,0:T(4,128)S(1)}, f32[118,4,128]{2,1,0:T(4,128)S(1)}, u32[]{:S(2)}, u32[]{:S(2)}) collective-permute-start(f32[118,4,128]{2,1,0:T(4,128)S(1)} %get-tuple-element.12), channel_id=1, source_target_pairs={{0,24},{8,0},{16,8},{24,16},{1,25},{9,1},{17,9},{25,17},{2,26},{10... | collective-permute-start | bytes 725000 | tf_op jit(solution)/shard_map/ppermute | solution.py:324
  12.8 1.0 %collective-permute-start.2 = (f32[118,4,128]{2,1,0:T(4,128)S(1)}, f32[118,4,128]{2,1,0:T(4,128)S(1)}, u32[]{:S(2)}, u32[]{:S(2)}) collective-permute-start(f32[118,4,128]{2,1,0:T(4,128)S(1)} %get-tuple-element.10), channel_id=1, source_target_pairs={{0,8},{8,16},{16,24},{24,0},{1,9},{9,17},{17,25},{25,1},{2,10},{10... | collective-permute-start | bytes 725000 | tf_op jit(solution)/shard_map/ppermute | solution.py:324
  13.9 0.7 pad_maximum_fusion.1.ratio_ref
  14.6 4.5 %collective-permute-done.refs_3_ = f32[118,4,128]{2,1,0:T(4,128)S(1)} collective-permute-done((f32[118,4,128]{2,1,0:T(4,128)S(1)}, f32[118,4,128]{2,1,0:T(4,128)S(1)}, u32[]{:S(2)}, u32[]{:S(2)}) %collective-permute-start) | collective-permute-done | bytes 241696 | tf_op jit(solution)/shard_map/ppermute | solution.py:324
  19.1 14.3 %collective-permute-done.1.refs_2_ = f32[118,4,128]{2,1,0:T(4,128)S(1)} collective-permute-done((f32[118,4,128]{2,1,0:T(4,128)S(1)}, f32[118,4,128]{2,1,0:T(4,128)S(1)}, u32[]{:S(2)}, u32[]{:S(2)}) %collective-permute-start.1) | collective-permute-done | bytes 241696 | tf_op jit(solution)/shard_map/ppermute | solution.py:324
  33.4 0.7 reshape.89.vol_ref
  34.2 0.7 reshape.91.regress_ref
  35.6 37.4 %sweep.1 = (f32[40,1,80]{2,1,0:T(1,128)}, f32[4,128]{1,0:T(4,128)}) custom-call(s32[1]{0:T(128)} %bitcast.place_ref, f32[3200]{0:T(1024)} %reshape.89.vol_ref, f32[400]{0:T(512)} %pad_maximum_fusion.1.ratio_ref, f32[240]{0:T(256)} %reshape.91.regress_ref, s32[40]{0:T(128)} %convert_element_type.16.slot_ref, f32[80]{0:T(128)} %curve_ref.1, ...), custom_call_target="tpu_custom_call" | custom-call | tf_op jit(solution)/shard_map/sweep/pallas_call | solution.py:411
  73.4 1.4 %reduce.11 = f32[40,80]{1,0:T(8,128)S(1)} reduce(f32[40,1,80]{2,1,0:T(1,128)} %get-tuple-element.4, f32[]{:T(128)} %broadcast.47), dimensions={1}, to_apply=%get-tuple-element.4.reduce_sub_computation.3 | reduce | bytes 25604 | tf_op jit(solution)/shard_map/sweep/pallas_call | solution.py:411
  75.0 0.7 copy-done.9
  75.9 2.8 %collective-permute-start.4 = (f32[1312]{0:T(1024)S(1)}, f32[1312]{0:T(1024)S(1)}, u32[]{:S(2)}, u32[]{:S(2)}) collective-permute-start(f32[1312]{0:T(1024)S(1)} %get-tuple-element.8), channel_id=1, source_target_pairs={{0,16},{8,24},{16,0},{24,8},{1,17},{9,25},{17,1},{25,9},{2,18},{10... | collective-permute-start | bytes 15752 | tf_op jit(solution)/shard_map/ppermute | solution.py:324
  78.7 1.9 %collective-permute-start.3 = (f32[1312]{0:T(1024)S(1)}, f32[1312]{0:T(1024)S(1)}, u32[]{:S(2)}, u32[]{:S(2)}) collective-permute-start(f32[1312]{0:T(1024)S(1)} %get-tuple-element.6), channel_id=1, source_target_pairs={{0,8},{8,16},{16,24},{24,0},{1,9},{9,17},{17,25},{25,1},{2,10},{10... | collective-permute-start | bytes 15752 | tf_op jit(solution)/shard_map/ppermute | solution.py:324
  80.9 3.2 %collective-permute-done.3 = f32[1312]{0:T(1024)S(1)} collective-permute-done((f32[1312]{0:T(1024)S(1)}, f32[1312]{0:T(1024)S(1)}, u32[]{:S(2)}, u32[]{:S(2)}) %collective-permute-start.3) | collective-permute-done | bytes 5280 | tf_op jit(solution)/shard_map/ppermute | solution.py:324
  84.3 1.2 %collective-permute-done.6 = f32[10,80]{1,0:T(8,128)S(1)} collective-permute-done((f32[10,80]{1,0:T(8,128)S(1)}, f32[10,80]{1,0:T(8,128)S(1)}, u32[]{:S(2)}, u32[]{:S(2)}) %collective-permute-start.6) | collective-permute-done | bytes 3232 | tf_op jit(solution)/shard_map/ppermute | solution.py:335
  85.5 1.5 %collective-permute-start.7 = (f32[10,80]{1,0:T(8,128)S(1)}, f32[10,80]{1,0:T(8,128)S(1)}, u32[]{:S(2)}, u32[]{:S(2)}) collective-permute-start(f32[10,80]{1,0:T(8,128)S(1)} %add.89), channel_id=1, source_target_pairs={{0,2},{1,3},{2,0},{3,1},{4,6},{5,7},{6,4},{7,5},{8,10},{9,11},{10,... | collective-permute-start | bytes 9608 | tf_op jit(solution)/shard_map/ppermute | solution.py:335
  87.3 1.8 %collective-permute-done.7 = f32[10,80]{1,0:T(8,128)S(1)} collective-permute-done((f32[10,80]{1,0:T(8,128)S(1)}, f32[10,80]{1,0:T(8,128)S(1)}, u32[]{:S(2)}, u32[]{:S(2)}) %collective-permute-start.7) | collective-permute-done | bytes 3232 | tf_op jit(solution)/shard_map/ppermute | solution.py:335
  89.1 1.5 %collective-permute-start.8 = (f32[10,80]{1,0:T(8,128)S(1)}, f32[10,80]{1,0:T(8,128)S(1)}, u32[]{:S(2)}, u32[]{:S(2)}) collective-permute-start(f32[10,80]{1,0:T(8,128)S(1)} %add.90), channel_id=1, source_target_pairs={{0,4},{1,5},{2,6},{3,7},{4,0},{5,1},{6,2},{7,3},{8,12},{9,13},{10,... | collective-permute-start | bytes 9608 | tf_op jit(solution)/shard_map/ppermute | solution.py:335
  91.3 1.5 %collective-permute-done.8 = f32[10,80]{1,0:T(8,128)S(1)} collective-permute-done((f32[10,80]{1,0:T(8,128)S(1)}, f32[10,80]{1,0:T(8,128)S(1)}, u32[]{:S(2)}, u32[]{:S(2)}) %collective-permute-start.8) | collective-permute-done | bytes 3232 | tf_op jit(solution)/shard_map/ppermute | solution.py:335
  92.8 0.7 multiply_select_fusion
  (80 shorter events, 5.6 us)
Async XLA Ops:
  1.9 0.9 copy-start.3
  2.9 1.0 %slice-start = ((f32[1,80,2048]{2,1,0:T(8,128)}), f32[1,64,2048]{2,1,0:T(8,128)S(1)}, s32[]{:S(2)}) async-start(f32[1,80,2048]{2,1,0:T(8,128)} %param.17), calls=%async_computation | async-start | bytes 1048576 | tf_op jit(solution)/shard_map/slice | solution.py:376
  3.9 0.7 copy-start.10
  3.9 0.7 copy-start.8
  4.6 0.7 copy-start.4
  5.4 0.7 copy-start.6
  6.1 0.7 copy-start.7
  7.7 6.1 %copy-start.5 = (f32[4,80]{1,0:T(4,128)S(1)}, f32[4,80]{1,0:T(4,128)}, u32[]{:S(2)}) copy-start(f32[4,80]{1,0:T(4,128)} %param.11) | copy-start | bytes 3844
  7.7 11.4 %collective-permute-start = (f32[118,4,128]{2,1,0:T(4,128)S(1)}, f32[118,4,128]{2,1,0:T(4,128)S(1)}, u32[]{:S(2)}, u32[]{:S(2)}) collective-permute-start(f32[118,4,128]{2,1,0:T(4,128)S(1)} %get-tuple-element.12), channel_id=1, source_target_pairs={{0,24},{8,0},{16,8},{24,16},{1,25},{9,1},{17,9},{25,17},{2,26},{10... | collective-permute-start | bytes 725000 | tf_op jit(solution)/shard_map/ppermute | solution.py:324
  12.8 20.6 %collective-permute-start.1 = (f32[118,4,128]{2,1,0:T(4,128)S(1)}, f32[118,4,128]{2,1,0:T(4,128)S(1)}, u32[]{:S(2)}, u32[]{:S(2)}) collective-permute-start(f32[118,4,128]{2,1,0:T(4,128)S(1)} %get-tuple-element.11), channel_id=1, source_target_pairs={{0,16},{8,24},{16,0},{24,8},{1,17},{9,25},{17,1},{25,9},{2,18},{10... | collective-permute-start | bytes 725000 | tf_op jit(solution)/shard_map/ppermute | solution.py:324
  12.8 20.6 %collective-permute-start.2 = (f32[118,4,128]{2,1,0:T(4,128)S(1)}, f32[118,4,128]{2,1,0:T(4,128)S(1)}, u32[]{:S(2)}, u32[]{:S(2)}) collective-permute-start(f32[118,4,128]{2,1,0:T(4,128)S(1)} %get-tuple-element.10), channel_id=1, source_target_pairs={{0,8},{8,16},{16,24},{24,0},{1,9},{9,17},{17,25},{25,1},{2,10},{10... | collective-permute-start | bytes 725000 | tf_op jit(solution)/shard_map/ppermute | solution.py:324
  19.1 16.5 %copy-start = (f32[118,4,128]{2,1,0:T(4,128)}, f32[118,4,128]{2,1,0:T(4,128)S(1)}, u32[]{:S(2)}) copy-start(f32[118,4,128]{2,1,0:T(4,128)S(1)} %collective-permute-done.refs_3_) | copy-start | bytes 724996
  33.3 2.2 %copy-start.1 = (f32[118,4,128]{2,1,0:T(4,128)}, f32[118,4,128]{2,1,0:T(4,128)S(1)}, u32[]{:S(2)}) copy-start(f32[118,4,128]{2,1,0:T(4,128)S(1)} %collective-permute-done.1.refs_2_) | copy-start | bytes 724996
  33.3 2.2 %copy-start.2 = (f32[118,4,128]{2,1,0:T(4,128)}, f32[118,4,128]{2,1,0:T(4,128)S(1)}, u32[]{:S(2)}) copy-start(f32[118,4,128]{2,1,0:T(4,128)S(1)} %collective-permute-done.2.refs_1_) | copy-start | bytes 724996
  75.0 0.7 copy-start.9
  75.8 5.0 %collective-permute-start.5 = (f32[1312]{0:T(1024)S(1)}, f32[1312]{0:T(1024)S(1)}, u32[]{:S(2)}, u32[]{:S(2)}) collective-permute-start(f32[1312]{0:T(1024)S(1)} %get-tuple-element.7), channel_id=1, source_target_pairs={{0,24},{8,0},{16,8},{24,16},{1,25},{9,1},{17,9},{25,17},{2,26},{10... | collective-permute-start | bytes 15752 | tf_op jit(solution)/shard_map/ppermute | solution.py:324
  75.9 5.0 %collective-permute-start.4 = (f32[1312]{0:T(1024)S(1)}, f32[1312]{0:T(1024)S(1)}, u32[]{:S(2)}, u32[]{:S(2)}) collective-permute-start(f32[1312]{0:T(1024)S(1)} %get-tuple-element.8), channel_id=1, source_target_pairs={{0,16},{8,24},{16,0},{24,8},{1,17},{9,25},{17,1},{25,9},{2,18},{10... | collective-permute-start | bytes 15752 | tf_op jit(solution)/shard_map/ppermute | solution.py:324
  78.7 5.4 %collective-permute-start.3 = (f32[1312]{0:T(1024)S(1)}, f32[1312]{0:T(1024)S(1)}, u32[]{:S(2)}, u32[]{:S(2)}) collective-permute-start(f32[1312]{0:T(1024)S(1)} %get-tuple-element.6), channel_id=1, source_target_pairs={{0,8},{8,16},{16,24},{24,0},{1,9},{9,17},{17,25},{25,1},{2,10},{10... | collective-permute-start | bytes 15752 | tf_op jit(solution)/shard_map/ppermute | solution.py:324
  84.2 1.2 %collective-permute-start.6 = (f32[10,80]{1,0:T(8,128)S(1)}, f32[10,80]{1,0:T(8,128)S(1)}, u32[]{:S(2)}, u32[]{:S(2)}) collective-permute-start(f32[10,80]{1,0:T(8,128)S(1)} %add_add_fusion), channel_id=1, source_target_pairs={{0,1},{1,0},{2,3},{3,2},{4,5},{5,4},{6,7},{7,6},{8,9},{9,8},{10,11... | collective-permute-start | bytes 9608 | tf_op jit(solution)/shard_map/ppermute | solution.py:335
  85.5 3.7 %collective-permute-start.7 = (f32[10,80]{1,0:T(8,128)S(1)}, f32[10,80]{1,0:T(8,128)S(1)}, u32[]{:S(2)}, u32[]{:S(2)}) collective-permute-start(f32[10,80]{1,0:T(8,128)S(1)} %add.89), channel_id=1, source_target_pairs={{0,2},{1,3},{2,0},{3,1},{4,6},{5,7},{6,4},{7,5},{8,10},{9,11},{10,... | collective-permute-start | bytes 9608 | tf_op jit(solution)/shard_map/ppermute | solution.py:335
  89.1 3.7 %collective-permute-start.8 = (f32[10,80]{1,0:T(8,128)S(1)}, f32[10,80]{1,0:T(8,128)S(1)}, u32[]{:S(2)}, u32[]{:S(2)}) collective-permute-start(f32[10,80]{1,0:T(8,128)S(1)} %add.90), channel_id=1, source_target_pairs={{0,4},{1,5},{2,6},{3,7},{4,0},{5,1},{6,2},{7,3},{8,12},{9,13},{10,... | collective-permute-start | bytes 9608 | tf_op jit(solution)/shard_map/ppermute | solution.py:335

commit v2 on v1

--- a/solution.py
+++ b/solution.py
@@ -12,7 +12,8 @@
 SMOOTHING = 0.01
 NOTIONAL = 100.0
 LANES = 128
-BLOCK = 8
+BLOCK = 16
+LOG2E = 1.4426950408889634
 
 
 def kernel(
@@ -22,6 +23,7 @@
     regress_ref,
     slot_ref,
     curve_ref,
+    scale_ref,
     *refs,
     shards,
     per_shard,
@@ -35,13 +37,8 @@
     (
         inbox,
         rate,
-        disc,
-        res_growth,
-        res_exp,
-        res_slope,
+        res_disc,
         res_tilt,
-        res_drive,
-        res_disc,
         res_sum,
         grads,
         annuities,
@@ -66,6 +63,7 @@
     row_rates = row_flag + per_shard
     row_numer = row_rates + forwards - low_row
     row_survive = row_numer + 1
+    lowest = [max(0, 2 * s * per_shard - 1) // BLOCK for s in range(shards)]
 
     def fetch(step):
         source = lax.rem(place - step + shards, shards)
@@ -76,102 +74,95 @@
     for step in range(shards):
         fetch(step).wait()
 
-    def first_block(opening):
-        return opening // BLOCK
+    def horizon_of(date):
+        return jnp.where(date == 0, ACCRUAL, 2.0 * ACCRUAL)
 
     def forward_date(shard, offset, carry):
         pos, numer = carry
         date = shard * per_shard + offset
         opening = 2 * date + 1
         is_start = date == 0
-        horizon = jnp.where(is_start, ACCRUAL, 2.0 * ACCRUAL)
+        horizon = horizon_of(date)
         inv_root = jnp.where(is_start, ACCRUAL**-0.5, (2.0 * ACCRUAL) ** -0.5)
         near = jnp.maximum(opening - 2, 0)
         last = opening - 1
-        numer = numer * (1.0 + rate[last])
-        numer = numer * jnp.where(is_start, 1.0, 1.0 + rate[near])
+        before = pos - blocks
+        numer = numer * (1.0 + rate[shard, last])
+        numer = numer * jnp.where(is_start, 1.0, 1.0 + rate[shard, near])
         numers[date] = numer
-        fixes[2 * date] = disc[near]
-        fixes[2 * date + 1] = disc[last]
+        fixes[2 * date] = 1.0 - res_disc[before * BLOCK + near]
+        fixes[2 * date + 1] = 1.0 - res_disc[before * BLOCK + last]
         sums = tuple(inbox[shard, offset * factors + f] * inv_root for f in range(factors))
+        begin = opening // BLOCK
+        shift = pos - begin
 
         def one_block(block, state, masked):
-            pos, sums, bond, total = state
+            sums, bond, total = state
             sums = list(sums)
+            olds = [res_disc[(before + block) * BLOCK + inner] for inner in range(BLOCK)]
+            rates = [rate[shard, block * BLOCK + inner] for inner in range(BLOCK)]
+            kept = []
             for inner in range(BLOCK):
                 row = block * BLOCK + inner
-                at = pos * BLOCK + inner
                 vol = vol_ref[date * forwards + row]
                 if masked:
                     alive = row >= opening
                     vol = jnp.where(alive, vol, 0.0)
                 lead = vol * ratio_ref[row]
                 half = vol * ratio_ref[forwards + row]
-                timed = horizon * lead
-                old = disc[row]
-                drive = lead * (1.0 - old)
+                timed = (horizon * LOG2E) * lead
+                drive = lead * (1.0 - olds[inner])
                 sums[0] = sums[0] + drive
                 tilt = sums[0]
                 for f in range(1, factors):
-                    scale = ratio_ref[(f + 1) * forwards + row]
+                    scale = scale_ref[(f - 1) * forwards + row]
                     sums[f] = sums[f] + scale * drive
                     tilt = tilt + scale * sums[f]
                 tilt = tilt - half
-                grow = jnp.exp(timed * tilt)
-                new = rate[row] * grow
+                new = rates[inner] * jnp.exp2(timed * tilt)
                 fresh = 1.0 / (1.0 + new)
-                rate[row] = new
-                disc[row] = fresh
-                res_growth[at] = timed * new
-                res_exp[at] = grow
-                res_slope[at] = lead * (old * old)
-                res_tilt[at] = tilt - half
-                res_drive[at] = drive
-                res_sum[at] = total
                 if masked:
-                    mask = alive.astype(jnp.float32)
-                    res_disc[at] = fresh * mask
-                    bond = bond * jnp.where(alive, fresh, 1.0)
-                    total = total + bond * mask
-                else:
-                    res_disc[at] = fresh
-                    bond = bond * fresh
-                    total = total + bond
-            return (pos + 1, tuple(sums), bond, total)
-
-        begin = first_block(opening)
+                    fresh = jnp.where(alive, fresh, 1.0)
+                kept.append((new, fresh, tilt - half, total))
+                bond = bond * fresh
+                total = total + (jnp.where(alive, bond, 0.0) if masked else bond)
+            for inner, (new, fresh, lean, total_before) in enumerate(kept):
+                at = (shift + block) * BLOCK + inner
+                rate[shard, block * BLOCK + inner] = new
+                res_disc[at] = fresh
+                res_tilt[at] = lean
+                res_sum[at] = total_before
+            return (tuple(sums), bond, total)
+
         state = one_block(
-            begin, (pos, sums, jnp.ones(tile, jnp.float32), jnp.zeros(tile, jnp.float32)), True
+            begin, (sums, jnp.ones(tile, jnp.float32), jnp.zeros(tile, jnp.float32)), True
         )
-        pos, _, bond, total = lax.fori_loop(
+        _, bond, total = lax.fori_loop(
             begin + 1, blocks, lambda block, s: one_block(block, s, False), state
         )
         annuities[date] = ACCRUAL * total
         finals[date] = bond
-        return (pos, numer)
+        return (pos + blocks - begin, numer)
 
     pos = jnp.int32(0)
     ends = []
     for shard in range(shards):
+        skip = lowest[shard]
+
+        def fill(row, pos, shard=shard, skip=skip):
+            if shard == 0:
+                start = jnp.full(tile, ACCRUAL * curve_ref[row], jnp.float32)
+            else:
+                start = ACCRUAL * inbox[shard - 1, row_rates + row - low_row]
+            rate[shard, row] = start
+            res_disc[(pos - skip) * BLOCK + row] = 1.0 / (1.0 + start)
+            return pos
+
+        lax.fori_loop(skip * BLOCK, forwards, fill, pos, unroll=BLOCK)
+        pos = pos + blocks - skip
         if shard == 0:
-            def fill(row, _):
-                start = jnp.full(tile, ACCRUAL * curve_ref[row], jnp.float32)
-                rate[row] = start
-                disc[row] = 1.0 / (1.0 + start)
-                return 0
-
-            lax.fori_loop(0, forwards, fill, 0, unroll=BLOCK)
             numer = jnp.ones(tile, jnp.float32)
         else:
-            lowest = (2 * shard * per_shard - 1) // BLOCK * BLOCK
-
-            def fill(row, _, shard=shard):
-                start = ACCRUAL * inbox[shard - 1, row_rates + row - low_row]
-                rate[row] = start
-                disc[row] = 1.0 / (1.0 + start)
-                return 0
-
-            lax.fori_loop(lowest, forwards, fill, 0, unroll=BLOCK)
             numer = inbox[shard - 1, row_numer]
         pos, numer = lax.fori_loop(
             0, per_shard, functools.partial(forward_date, shard), (pos, numer)
@@ -249,59 +240,84 @@
 
     lax.fori_loop(0, forwards, clear, 0, unroll=BLOCK)
 
-    def backward_date(step, pos):
-        date = dates - 1 - step
+    def backward_date(shard, step, pos):
+        date = shard * per_shard + per_shard - 1 - step
         opening = 2 * date + 1
+        horizon = horizon_of(date)
         seed_level = seeds_b[2 * date]
         seed_slope = seeds_b[2 * date + 1]
-
-        def one_block(back, state):
-            pos, sums = state
+        begin = opening // BLOCK
+        here = pos - blocks
+        before = here - (blocks - begin)
+
+        def one_block(back, sums):
             sums = list(sums)
             block = blocks - 1 - back
-            pos = pos - 1
+            laters = [adjoint[block * BLOCK + inner] for inner in range(BLOCK)]
+            kept = []
             for inner in reversed(range(BLOCK)):
                 row = block * BLOCK + inner
-                at = pos * BLOCK + inner
-                pull = (seed_level - seed_slope * res_sum[at]) * res_disc[at]
-                inward = adjoint[row] - pull
-                timed = inward * res_growth[at]
+                at = (here + block) * BLOCK + inner
+                lead = vol_ref[date * forwards + row] * ratio_ref[row]
+                old = res_disc[(before + block) * BLOCK + inner]
+                pull = (seed_level - seed_slope * res_sum[at]) * (1.0 - res_disc[at])
+                inward = laters[inner] - pull
+                timed = (horizon * lead) * inward
                 sums[0] = sums[0] + timed
                 drive_adj = sums[0]
                 for f in range(1, factors):
-                    scale = ratio_ref[(f + 1) * forwards + row]
+                    scale = scale_ref[(f - 1) * forwards + row]
                     sums[f] = sums[f] + scale * timed
                     drive_adj = drive_adj + scale * sums[f]
-                adjoint[row] = inward * res_exp[at] + drive_adj * res_slope[at]
-                grads[date * forwards + row] = timed * res_tilt[at] + drive_adj * res_drive[at]
-            return (pos, tuple(sums))
+                drive_adj = lead * drive_adj
+                part = drive_adj * old
+                kept.append(
+                    (row, inward + (part - part * old), timed * res_tilt[at] + (drive_adj - part))
+                )
+            for row, earlier, grad in kept:
+                adjoint[row] = earlier
+                grads[pl.ds((date * forwards + row) * sub, sub)] = grad
+            return tuple(sums)
 
         zero = jnp.zeros(tile, jnp.float32)
-        pos, _ = lax.fori_loop(
-            0, blocks - first_block(opening), one_block, (pos, (zero,) * factors)
-        )
+        lax.fori_loop(0, blocks - begin, one_block, (zero,) * factors)
         near = jnp.maximum(opening - 2, 0)
         last = opening - 1
         level = numer_adj[date]
         adjoint[near] = level * fixes[2 * date]
         adjoint[last] = level * fixes[2 * date + 1]
-        return pos
-
-    lax.fori_loop(0, dates, backward_date, pos)
-
-    ones = jnp.ones((BLOCK, LANES), jnp.float32)
+        return pos - (blocks - begin)
+
+    for shard in reversed(range(shards)):
+        pos = lax.fori_loop(0, per_shard, functools.partial(backward_date, shard), pos)
+        pos = pos - (blocks - lowest[shard])
+        if shard > 0:
+
+            def cross(row, _, shard=shard):
+                start = ACCRUAL * inbox[shard - 1, row_rates + row - low_row]
+                adjoint[row] = adjoint[row] * rate[shard - 1, row] / start
+                return 0
+
+            lax.fori_loop(2 * shard * per_shard - 1, forwards, cross, 0)
+
+    ones = jnp.ones((8, LANES), jnp.bfloat16)
+    width = forwards * sub
+
+    def along(picked):
+        return lax.dot_general(
+            ones, picked, (((1,), (1,)), ((), ())), preferred_element_type=jnp.float32
+        )
 
     def collect(date, _):
-        picked = grads[pl.ds(date * forwards, forwards)]
-        summed = jnp.sum(picked, axis=1)
-        row = lax.dot_general(
-            ones, summed, (((1,), (1,)), ((), ())),
-            precision=lax.Precision.HIGHEST, preferred_element_type=jnp.float32,
-        )
-        vega_ref[date] = row[0:1]
+        picked = grads[pl.ds(date * width, forwards, stride=sub)]
+        for q in range(1, sub):
+            picked = picked + grads[pl.ds(date * width + q, forwards, stride=sub)]
+        top = picked.astype(jnp.bfloat16)
+        rest = (picked - top.astype(jnp.float32)).astype(jnp.bfloat16)
+        vega_ref[pl.ds(date, 1)] = (along(top) + along(rest))[0:1]
         return 0
 
-    lax.fori_loop(0, dates, collect, 0)
+    lax.fori_loop(0, dates, collect, 0, unroll=4)
 
 
 def turned(parts, start):
@@ -396,14 +412,17 @@
         .astype(jnp.int32)
     )
     loads = loadings / jnp.sqrt(jnp.sum(loadings * loadings, axis=0, keepdims=True))
-    ratios = jnp.concatenate([loads[0], 0.5 / loads[0], (loads[1:] / loads[:1]).reshape(-1)])
-
-    triangle = sum(
-        forwards // BLOCK - min((2 * d + 1) // BLOCK, forwards // BLOCK - 1) for d in range(dates)
-    )
+    ratios = jnp.concatenate([loads[0], 0.5 / loads[0]])
+    scales = jnp.broadcast_to(
+        (loads[1:] / loads[:1]).reshape(-1, 1, 1), ((factors - 1) * forwards, sub, LANES)
+    )
+
+    blocks = forwards // BLOCK
+    triangle = sum(blocks - (2 * d + 1) // BLOCK for d in range(dates))
+    starts = sum(blocks - max(0, 2 * s * per_shard - 1) // BLOCK for s in range(shards))
     tile = (sub, LANES)
     f32 = jnp.float32
-    residual = pltpu.VMEM((triangle * BLOCK,) + tile, f32)
+    residual = pltpu.VMEM(((triangle + starts) * BLOCK,) + tile, f32)
     per_date = pltpu.VMEM((dates,) + tile, f32)
     two_per_date = pltpu.VMEM((2 * dates,) + tile, f32)
     per_forward = pltpu.VMEM((forwards,) + tile, f32)
@@ -419,26 +438,23 @@
             low_row=low_row,
         ),
         out_shape=(
-            jax.ShapeDtypeStruct((dates, 1, forwards), f32),
+            jax.ShapeDtypeStruct((dates, forwards), f32),
             jax.ShapeDtypeStruct(tile, f32),
         ),
-        in_specs=[smem] * 6 + [pl.BlockSpec(memory_space=pl.ANY)] * shards,
+        in_specs=[smem] * 6
+        + [pl.BlockSpec(memory_space=pltpu.VMEM)]
+        + [pl.BlockSpec(memory_space=pl.ANY)] * shards,
         out_specs=(
             pl.BlockSpec(memory_space=pltpu.VMEM),
             pl.BlockSpec(memory_space=pltpu.VMEM),
         ),
         scratch_shapes=[
             pltpu.VMEM((shards, rows) + tile, f32),
-            per_forward,
-            per_forward,
+            pltpu.VMEM((shards, forwards) + tile, f32),
             residual,
             residual,
             residual,
-            residual,
-            residual,
-            residual,
-            residual,
-            pltpu.VMEM((dates * forwards,) + tile, f32),
+            pltpu.VMEM((dates * forwards * sub, LANES), f32),
             per_date,
             per_date,
             per_date,
@@ -461,6 +477,7 @@
         regress_all,
         slot_all,
         start_curve,
+        scales,
         own,
         *received,
     )

time: 94 us -> 84.4 us (0.90)
  Pallas kernels: 37.4 us -> 27.9 us
  other arithmetic: 2.99 us -> 1.54 us
  local copies, waits for them, and re-layouts: 11.8 us -> 13.1 us
    pallas_call x1, Pallas kernels: 37.4 us -> 27.9 us  [local(): pl.pallas_call(functools.partial(kernel, shards=shards, per_shard=per_sha...]
    pallas_call x1 -> x0, other arithmetic: 1.43 us -> none  [local(): pl.pallas_call(functools.partial(kernel, shards=shards, per_shard=per_sha...]
    broadcast_in_dim x0 -> x2, local copies, waits for them, and re-layouts: none -> 1.19 us  [local(): jnp.broadcast_to((loads[1:] / loads[:1]).reshape(-1, 1, 1), ((factors - 1...]
where the time goes in v2:
time: 84.4 us; the launch traced here: 83.9 us
  Pallas kernels  27.9 us (33%)
  waiting for transfers between devices  26.5 us (31%)
  starting transfers between devices  14 us (17%)
  local copies, waits for them, and re-layouts  13.1 us (16%)
  other arithmetic  1.54 us (2%)
  between operations  0.86 us (1%)
    pallas_call x1, Pallas kernels, local(): pl.pallas_call(functools.partial(kernel, shards=shards, per_shard=per_sha...  27.9 us
    ppermute x6, waiting for transfers between devices, exchange(): lax.ppermute(sent, axis, [(s, (s + step) % count) for s in range(count)])  22 us
    ppermute x6, starting transfers between devices, exchange(): lax.ppermute(sent, axis, [(s, (s + step) % count) for s in range(count)])  10.9 us
    unnamed x30, local copies, waits for them, and re-layouts  4.56 us
    ppermute x3, waiting for transfers between devices, total_over(): lax.ppermute(value, axis, [(s, s ^ step) for s in range(count)])  4.5 us
    ppermute x3, starting transfers between devices, total_over(): lax.ppermute(value, axis, [(s, s ^ step) for s in range(count)])  3.08 us
  transfers between devices with their start and end apart: 9, of which 6 were waited for; matrix products, arithmetic and copies ran while one was open for 2% of the time, Pallas kernels for 0%

profile of v2, /device:TPU:0, one launch (start us, length us, event | category | flops | bytes accessed | tf_op | source)
XLA Modules:
  0.0 83.9 jit_solution(551812162882218730)
XLA Ops:
  0.6 1.2 %reshape_reshape.3 = f32[40,4,4,128]{3,2,1,0:T(4,128)S(1)} reshape(f32[10,4,2048]{2,1,0:T(4,128)} %param.13) | data formatting | bytes 655360 | tf_op jit(solution)/shard_map/reshape;reshape | solution.py:381
  2.0 0.8 copy-done.3
  2.9 1.0 %slice-done = f32[1,64,2048]{2,1,0:T(8,128)S(1)} async-done(((f32[1,80,2048]{2,1,0:T(8,128)}), f32[1,64,2048]{2,1,0:T(8,128)S(1)}, s32[]{:S(2)}) %slice-start) | async-done | bytes 524312 | tf_op jit(solution)/shard_map/slice | solution.py:392
  6.1 0.7 copy-done.7
  6.9 0.8 dynamic-slice_bitcast_fusion.3
  7.7 5.1 %collective-permute-start = (f32[118,4,128]{2,1,0:T(4,128)S(1)}, f32[118,4,128]{2,1,0:T(4,128)S(1)}, u32[]{:S(2)}, u32[]{:S(2)}) collective-permute-start(f32[118,4,128]{2,1,0:T(4,128)S(1)} %get-tuple-element.12), channel_id=1, source_target_pairs={{0,24},{8,0},{16,8},{24,16},{1,25},{9,1},{17,9},{25,17},{2,26},{10... | collective-permute-start | bytes 725000 | tf_op jit(solution)/shard_map/ppermute | solution.py:340
  12.8 1.0 %collective-permute-start.2 = (f32[118,4,128]{2,1,0:T(4,128)S(1)}, f32[118,4,128]{2,1,0:T(4,128)S(1)}, u32[]{:S(2)}, u32[]{:S(2)}) collective-permute-start(f32[118,4,128]{2,1,0:T(4,128)S(1)} %get-tuple-element.10), channel_id=1, source_target_pairs={{0,8},{8,16},{16,24},{24,0},{1,9},{9,17},{17,25},{25,1},{2,10},{10... | collective-permute-start | bytes 725000 | tf_op jit(solution)/shard_map/ppermute | solution.py:340
  14.6 4.5 %collective-permute-done.refs_3_ = f32[118,4,128]{2,1,0:T(4,128)S(1)} collective-permute-done((f32[118,4,128]{2,1,0:T(4,128)S(1)}, f32[118,4,128]{2,1,0:T(4,128)S(1)}, u32[]{:S(2)}, u32[]{:S(2)}) %collective-permute-start) | collective-permute-done | bytes 241696 | tf_op jit(solution)/shard_map/ppermute | solution.py:340
  19.1 14.3 %collective-permute-done.1.refs_2_ = f32[118,4,128]{2,1,0:T(4,128)S(1)} collective-permute-done((f32[118,4,128]{2,1,0:T(4,128)S(1)}, f32[118,4,128]{2,1,0:T(4,128)S(1)}, u32[]{:S(2)}, u32[]{:S(2)}) %collective-permute-start.1) | collective-permute-done | bytes 241696 | tf_op jit(solution)/shard_map/ppermute | solution.py:340
  33.4 0.7 reshape.88.vol_ref
  34.9 0.7 convert_element_type.16.slot_ref
  35.6 1.1 %broadcast_in_dim.31.scale_ref = f32[240,4,128]{2,1,0:T(4,128)} broadcast(f32[240]{0:T(256)S(1)} %broadcast_in_dim.30), dimensions={0} | broadcast | bytes 492480 | tf_op jit(solution)/shard_map/broadcast_in_dim | solution.py:416
  36.7 27.9 %sweep.1 = (f32[40,80]{1,0:T(8,128)}, f32[4,128]{1,0:T(4,128)}) custom-call(s32[1]{0:T(128)} %bitcast.place_ref, f32[3200]{0:T(1024)} %reshape.88.vol_ref, f32[160]{0:T(256)} %pad_maximum_fusion.1.ratio_ref, f32[240]{0:T(256)} %reshape.89.regress_ref, s32[40]{0:T(128)} %convert_element_type.16.slot_ref, f32[80]{0:T(128)} %curve_ref.1, ...), custom_call_target="tpu_custom_call" | custom-call | tf_op jit(solution)/shard_map/sweep/pallas_call | solution.py:430
  64.6 0.8 reshape.90
  65.4 0.7 copy-done.9
  66.3 2.8 %collective-permute-start.4 = (f32[1312]{0:T(1024)S(1)}, f32[1312]{0:T(1024)S(1)}, u32[]{:S(2)}, u32[]{:S(2)}) collective-permute-start(f32[1312]{0:T(1024)S(1)} %get-tuple-element.8), channel_id=1, source_target_pairs={{0,16},{8,24},{16,0},{24,8},{1,17},{9,25},{17,1},{25,9},{2,18},{10... | collective-permute-start | bytes 15752 | tf_op jit(solution)/shard_map/ppermute | solution.py:340
  69.1 1.9 %collective-permute-start.3 = (f32[1312]{0:T(1024)S(1)}, f32[1312]{0:T(1024)S(1)}, u32[]{:S(2)}, u32[]{:S(2)}) collective-permute-start(f32[1312]{0:T(1024)S(1)} %get-tuple-element.6), channel_id=1, source_target_pairs={{0,8},{8,16},{16,24},{24,0},{1,9},{9,17},{17,25},{25,1},{2,10},{10... | collective-permute-start | bytes 15752 | tf_op jit(solution)/shard_map/ppermute | solution.py:340
  71.3 3.2 %collective-permute-done.3 = f32[1312]{0:T(1024)S(1)} collective-permute-done((f32[1312]{0:T(1024)S(1)}, f32[1312]{0:T(1024)S(1)}, u32[]{:S(2)}, u32[]{:S(2)}) %collective-permute-start.3) | collective-permute-done | bytes 5280 | tf_op jit(solution)/shard_map/ppermute | solution.py:340
  74.7 1.2 %collective-permute-done.6 = f32[10,80]{1,0:T(8,128)S(1)} collective-permute-done((f32[10,80]{1,0:T(8,128)S(1)}, f32[10,80]{1,0:T(8,128)S(1)}, u32[]{:S(2)}, u32[]{:S(2)}) %collective-permute-start.6) | collective-permute-done | bytes 3232 | tf_op jit(solution)/shard_map/ppermute | solution.py:351
  75.9 1.5 %collective-permute-start.7 = (f32[10,80]{1,0:T(8,128)S(1)}, f32[10,80]{1,0:T(8,128)S(1)}, u32[]{:S(2)}, u32[]{:S(2)}) collective-permute-start(f32[10,80]{1,0:T(8,128)S(1)} %add.89), channel_id=1, source_target_pairs={{0,2},{1,3},{2,0},{3,1},{4,6},{5,7},{6,4},{7,5},{8,10},{9,11},{10,... | collective-permute-start | bytes 9608 | tf_op jit(solution)/shard_map/ppermute | solution.py:351
  77.7 1.8 %collective-permute-done.7 = f32[10,80]{1,0:T(8,128)S(1)} collective-permute-done((f32[10,80]{1,0:T(8,128)S(1)}, f32[10,80]{1,0:T(8,128)S(1)}, u32[]{:S(2)}, u32[]{:S(2)}) %collective-permute-start.7) | collective-permute-done | bytes 3232 | tf_op jit(solution)/shard_map/ppermute | solution.py:351
  79.6 1.5 %collective-permute-start.8 = (f32[10,80]{1,0:T(8,128)S(1)}, f32[10,80]{1,0:T(8,128)S(1)}, u32[]{:S(2)}, u32[]{:S(2)}) collective-permute-start(f32[10,80]{1,0:T(8,128)S(1)} %add.90), channel_id=1, source_target_pairs={{0,4},{1,5},{2,6},{3,7},{4,0},{5,1},{6,2},{7,3},{8,12},{9,13},{10,... | collective-permute-start | bytes 9608 | tf_op jit(solution)/shard_map/ppermute | solution.py:351
  81.7 1.5 %collective-permute-done.8 = f32[10,80]{1,0:T(8,128)S(1)} collective-permute-done((f32[10,80]{1,0:T(8,128)S(1)}, f32[10,80]{1,0:T(8,128)S(1)}, u32[]{:S(2)}, u32[]{:S(2)}) %collective-permute-start.8) | collective-permute-done | bytes 3232 | tf_op jit(solution)/shard_map/ppermute | solution.py:351
  83.2 0.7 multiply_select_fusion
  (79 shorter events, 5.7 us)
Async XLA Ops:
  1.9 0.9 %copy-start.3 = (s32[10,2048]{1,0:T(8,128)S(1)}, s32[10,2048]{1,0:T(8,128)}, u32[]{:S(2)}) copy-start(s32[10,2048]{1,0:T(8,128)} %param.14) | copy-start | bytes 245764
  2.9 1.0 %slice-start = ((f32[1,80,2048]{2,1,0:T(8,128)}), f32[1,64,2048]{2,1,0:T(8,128)S(1)}, s32[]{:S(2)}) async-start(f32[1,80,2048]{2,1,0:T(8,128)} %param.17), calls=%async_computation | async-start | bytes 1048576 | tf_op jit(solution)/shard_map/slice | solution.py:392
  3.9 0.7 copy-start.10
  3.9 0.7 copy-start.8
  4.6 0.7 copy-start.4
  5.4 0.7 copy-start.6
  6.1 0.7 copy-start.7
  7.7 6.1 %copy-start.5 = (f32[4,80]{1,0:T(4,128)S(1)}, f32[4,80]{1,0:T(4,128)}, u32[]{:S(2)}) copy-start(f32[4,80]{1,0:T(4,128)} %param.11) | copy-start | bytes 3844
  7.7 11.4 %collective-permute-start = (f32[118,4,128]{2,1,0:T(4,128)S(1)}, f32[118,4,128]{2,1,0:T(4,128)S(1)}, u32[]{:S(2)}, u32[]{:S(2)}) collective-permute-start(f32[118,4,128]{2,1,0:T(4,128)S(1)} %get-tuple-element.12), channel_id=1, source_target_pairs={{0,24},{8,0},{16,8},{24,16},{1,25},{9,1},{17,9},{25,17},{2,26},{10... | collective-permute-start | bytes 725000 | tf_op jit(solution)/shard_map/ppermute | solution.py:340
  12.8 20.6 %collective-permute-start.1 = (f32[118,4,128]{2,1,0:T(4,128)S(1)}, f32[118,4,128]{2,1,0:T(4,128)S(1)}, u32[]{:S(2)}, u32[]{:S(2)}) collective-permute-start(f32[118,4,128]{2,1,0:T(4,128)S(1)} %get-tuple-element.11), channel_id=1, source_target_pairs={{0,16},{8,24},{16,0},{24,8},{1,17},{9,25},{17,1},{25,9},{2,18},{10... | collective-permute-start | bytes 725000 | tf_op jit(solution)/shard_map/ppermute | solution.py:340
  12.8 20.6 %collective-permute-start.2 = (f32[118,4,128]{2,1,0:T(4,128)S(1)}, f32[118,4,128]{2,1,0:T(4,128)S(1)}, u32[]{:S(2)}, u32[]{:S(2)}) collective-permute-start(f32[118,4,128]{2,1,0:T(4,128)S(1)} %get-tuple-element.10), channel_id=1, source_target_pairs={{0,8},{8,16},{16,24},{24,0},{1,9},{9,17},{17,25},{25,1},{2,10},{10... | collective-permute-start | bytes 725000 | tf_op jit(solution)/shard_map/ppermute | solution.py:340
  19.1 17.6 %copy-start = (f32[118,4,128]{2,1,0:T(4,128)}, f32[118,4,128]{2,1,0:T(4,128)S(1)}, u32[]{:S(2)}) copy-start(f32[118,4,128]{2,1,0:T(4,128)S(1)} %collective-permute-done.refs_3_) | copy-start | bytes 724996
  33.3 3.4 %copy-start.1 = (f32[118,4,128]{2,1,0:T(4,128)}, f32[118,4,128]{2,1,0:T(4,128)S(1)}, u32[]{:S(2)}) copy-start(f32[118,4,128]{2,1,0:T(4,128)S(1)} %collective-permute-done.1.refs_2_) | copy-start | bytes 724996
  33.3 3.4 %copy-start.2 = (f32[118,4,128]{2,1,0:T(4,128)}, f32[118,4,128]{2,1,0:T(4,128)S(1)}, u32[]{:S(2)}) copy-start(f32[118,4,128]{2,1,0:T(4,128)S(1)} %collective-permute-done.2.refs_1_) | copy-start | bytes 724996
  65.4 0.7 copy-start.9
  66.2 5.0 %collective-permute-start.5 = (f32[1312]{0:T(1024)S(1)}, f32[1312]{0:T(1024)S(1)}, u32[]{:S(2)}, u32[]{:S(2)}) collective-permute-start(f32[1312]{0:T(1024)S(1)} %get-tuple-element.7), channel_id=1, source_target_pairs={{0,24},{8,0},{16,8},{24,16},{1,25},{9,1},{17,9},{25,17},{2,26},{10... | collective-permute-start | bytes 15752 | tf_op jit(solution)/shard_map/ppermute | solution.py:340
  66.3 5.0 %collective-permute-start.4 = (f32[1312]{0:T(1024)S(1)}, f32[1312]{0:T(1024)S(1)}, u32[]{:S(2)}, u32[]{:S(2)}) collective-permute-start(f32[1312]{0:T(1024)S(1)} %get-tuple-element.8), channel_id=1, source_target_pairs={{0,16},{8,24},{16,0},{24,8},{1,17},{9,25},{17,1},{25,9},{2,18},{10... | collective-permute-start | bytes 15752 | tf_op jit(solution)/shard_map/ppermute | solution.py:340
  69.1 5.4 %collective-permute-start.3 = (f32[1312]{0:T(1024)S(1)}, f32[1312]{0:T(1024)S(1)}, u32[]{:S(2)}, u32[]{:S(2)}) collective-permute-start(f32[1312]{0:T(1024)S(1)} %get-tuple-element.6), channel_id=1, source_target_pairs={{0,8},{8,16},{16,24},{24,0},{1,9},{9,17},{17,25},{25,1},{2,10},{10... | collective-permute-start | bytes 15752 | tf_op jit(solution)/shard_map/ppermute | solution.py:340
  74.7 1.2 %collective-permute-start.6 = (f32[10,80]{1,0:T(8,128)S(1)}, f32[10,80]{1,0:T(8,128)S(1)}, u32[]{:S(2)}, u32[]{:S(2)}) collective-permute-start(f32[10,80]{1,0:T(8,128)S(1)} %add_add_fusion), channel_id=1, source_target_pairs={{0,1},{1,0},{2,3},{3,2},{4,5},{5,4},{6,7},{7,6},{8,9},{9,8},{10,11... | collective-permute-start | bytes 9608 | tf_op jit(solution)/shard_map/ppermute | solution.py:351
  75.9 3.7 %collective-permute-start.7 = (f32[10,80]{1,0:T(8,128)S(1)}, f32[10,80]{1,0:T(8,128)S(1)}, u32[]{:S(2)}, u32[]{:S(2)}) collective-permute-start(f32[10,80]{1,0:T(8,128)S(1)} %add.89), channel_id=1, source_target_pairs={{0,2},{1,3},{2,0},{3,1},{4,6},{5,7},{6,4},{7,5},{8,10},{9,11},{10,... | collective-permute-start | bytes 9608 | tf_op jit(solution)/shard_map/ppermute | solution.py:351
  79.6 3.7 %collective-permute-start.8 = (f32[10,80]{1,0:T(8,128)S(1)}, f32[10,80]{1,0:T(8,128)S(1)}, u32[]{:S(2)}, u32[]{:S(2)}) collective-permute-start(f32[10,80]{1,0:T(8,128)S(1)} %add.90), channel_id=1, source_target_pairs={{0,4},{1,5},{2,6},{3,7},{4,0},{5,1},{6,2},{7,3},{8,12},{9,13},{10,... | collective-permute-start | bytes 9608 | tf_op jit(solution)/shard_map/ppermute | solution.py:351

commit v3 on v0

v3 whole, which is shorter than its diff:
```python
import functools

import jax
import jax.numpy as jnp
from jax import lax
from jax.experimental import pallas as pl
from jax.experimental.pallas import tpu as pltpu
from jax.sharding import PartitionSpec as P

ACCRUAL = 0.25
STRIKE = 0.04
SMOOTHING = 0.01
NOTIONAL = 100.0
LANES = 128
BLOCK = 8
LOG2E = 1.4426950408889634


class Layout:
    def __init__(self, shards, per_shard, forwards, factors, basis, paths):
        self.shards = shards
        self.per_shard = per_shard
        self.forwards = forwards
        self.factors = factors
        self.basis = basis
        self.per_device = paths // shards
        self.sub = self.per_device // LANES
        self.pairs = -(-per_shard // 2)
        self.low_row = max(0, 2 * per_shard - 1)
        self.shock = 0
        self.flag = self.shock + 2 * self.pairs * factors
        self.rates = self.flag + 2 * self.pairs
        self.numer = self.rates + forwards - self.low_row
        self.survive = self.numer + 1
        small = self.survive + 1
        while (small * self.sub) % 8:
            small += 1
        self.small = small * self.sub
        self.regress_at = per_shard
        self.slot_at = per_shard + basis
        self.small_rows = per_shard + basis + 1
        total = -(-(self.small + self.small_rows) // 8) * 8
        self.flat = total
        self.blocks = forwards // BLOCK


def pack_kernel(place_ref, *refs, lay, count):
    sources = refs[:count]
    out_refs = refs[count : count + lay.shards]
    held = refs[count + lay.shards : 2 * count + lay.shards]
    arrived = refs[-1]
    copies = [
        pltpu.make_async_copy(source, target, arrived.at[index])
        for index, (source, target) in enumerate(zip(sources, held))
    ]
    for copy in copies:
        copy.start()
    for copy in copies:
        copy.wait()
    shock_ref, flag_ref, rate_ref, numer_ref, survive_ref, vol_ref, regress_ref, slot_ref = held
    place = place_ref[0]
    sub = lay.sub
    for step, out in enumerate(out_refs):
        target = lax.rem(place + step, lay.shards)
        for q in range(sub):
            lanes = pl.ds(pl.multiple_of(target * lay.per_device + q * LANES, LANES), LANES)
            for d in range(lay.per_shard):
                row = lay.shock + (d // 2) * lay.factors * 2 + d % 2
                out[pl.ds(row * sub + q, lay.factors, stride=2 * sub), :] = shock_ref[d, :, lanes]
            out[pl.ds(lay.flag * sub + q, lay.per_shard, stride=sub), :] = flag_ref[
                :, lanes
            ].astype(jnp.float32)
            out[
                pl.ds(lay.rates * sub + q, lay.forwards - lay.low_row, stride=sub), :
            ] = rate_ref[0, lay.low_row :, lanes]
            out[pl.ds(lay.numer * sub + q, 1), :] = numer_ref[:, lanes]
            out[pl.ds(lay.survive * sub + q, 1), :] = survive_ref[:, lanes]
        base = lay.small
        out[pl.ds(base, lay.per_shard), :] = jnp.zeros((lay.per_shard, LANES), jnp.float32)
        out[pl.ds(base, lay.per_shard), 0 : lay.forwards] = vol_ref[...]
        out[pl.ds(base + lay.regress_at, lay.basis), 0 : lay.per_shard] = regress_ref[...]
        out[pl.ds(base + lay.slot_at, 1), 0 : lay.per_shard] = slot_ref[...].astype(jnp.float32)


def sweep_kernel(place_ref, curve_ref, table_ref, *refs, lay):
    shards, per_shard, forwards = lay.shards, lay.per_shard, lay.forwards
    factors, basis, sub, blocks, pairs = lay.factors, lay.basis, lay.sub, lay.blocks, lay.pairs
    block_refs = refs[:shards]
    vega_ref, value_ref = refs[shards : shards + 2]
    (
        inbox,
        smalls,
        rate,
        disc,
        res_old,
        res_disc,
        res_tilt,
        res_sum,
        grads,
        annuities,
        finals,
        numers,
        near_fix,
        last_fix,
        float_seed,
        annuity_seed,
        level_seed,
        slope_seed,
        numer_adj,
        survs,
        chances,
        pays,
        adjoint,
        arrived,
        small_arrived,
    ) = refs[shards + 2 :]
    f32 = jnp.float32
    tile = (sub, LANES)
    pair_tile = (2 * sub, LANES)
    place = place_ref[0]
    odd = per_shard % 2
    span = blocks + 2
    state_rows = BLOCK * span * sub
    lowest = [max(0, 2 * s * per_shard - 1) for s in range(shards)]
    is_low = lax.broadcasted_iota(jnp.int32, pair_tile, 0) < sub

    def fetch(step):
        source = lax.rem(place - step + shards, shards)
        return pltpu.make_async_copy(block_refs[step], inbox.at[source], arrived.at[step])

    def fetch_small(step, row):
        source = lax.rem(place - step + shards, shards)
        spot = (source * lay.small_rows + row) * LANES
        return pltpu.make_async_copy(
            block_refs[step].at[lay.small + row],
            smalls.at[pl.ds(pl.multiple_of(spot, LANES), LANES)],
            small_arrived.at[step, row],
        )

    for step in range(shards):
        fetch(step).start()
        for row in range(lay.small_rows):
            fetch_small(step, row).start()

    def clear(ref):
        rows = ref.shape[0]

        def one(row, _):
            ref[pl.ds(pl.multiple_of(row * 8, 8), 8)] = jnp.zeros((8, LANES), f32)
            return 0

        lax.fori_loop(0, rows // 8, one, 0, unroll=8)

    clear(rate)
    clear(disc)
    clear(adjoint)

    for step in range(shards):
        fetch(step).wait()
        for row in range(lay.small_rows):
            fetch_small(step, row).wait()

    def mail(shard, row, count=1):
        return inbox[shard, pl.ds(row * sub, count * sub)]

    def place_of(row):
        if isinstance(row, int):
            return (row % BLOCK * span + blocks - row // BLOCK) * sub
        return (lax.rem(row, BLOCK) * span + blocks - lax.div(row, BLOCK)) * sub

    def state(ref, row, shard=0):
        return ref[pl.ds(shard * state_rows + place_of(row), sub)]

    def slot_of(shard, offset):
        return (shard * 2 * pairs + offset) * sub

    def both(low, high):
        return jnp.where(is_low, low, high)

    def horizons(date):
        return both(jnp.where(date == 0, ACCRUAL, 2.0 * ACCRUAL), 2.0 * ACCRUAL)

    def opening_pair(shard, offset):
        opening = 2 * (shard * per_shard + offset) + 1
        second = opening + 2
        if odd:
            second = jnp.where(offset + 1 < per_shard, second, 4 * forwards)
        return opening, second

    inner_of = [
        both(0, BLOCK) - inner for inner in range(BLOCK)
    ]

    def volatility(shard, offset, block, limit):
        base = (shard * lay.small_rows + offset) * LANES + block * BLOCK
        first = jnp.broadcast_to(block * BLOCK, pair_tile)
        found = []
        for inner in range(BLOCK):
            raw = both(smalls[base + inner], smalls[base + (LANES - BLOCK + inner)])
            found.append(jnp.where(first >= limit + inner_of[inner], raw, 0.0))
        return found

    def table(kind, row):
        return table_ref[kind * (forwards + BLOCK) + row]

    def forward_pair(shard, index, carry):
        pos, numer = carry
        offset = 2 * index
        date = shard * per_shard + offset
        opening, second = opening_pair(shard, offset)
        limit = both(opening, second)
        begin = opening // BLOCK
        horizon = horizons(date)
        timer = horizon * LOG2E
        root = both(jnp.where(date == 0, ACCRUAL**-0.5, (2.0 * ACCRUAL) ** -0.5), (2.0 * ACCRUAL) ** -0.5)
        sums = tuple(
            mail(shard, lay.shock + (index * factors + f) * 2, 2) * root for f in range(factors)
        )

        if odd:
            real = is_low | (offset + 1 < per_shard)
            sums = tuple(jnp.where(real, part, 0.0) for part in sums)

        def one_block(step, held):
            sums, bond, total = held
            sums = list(sums)
            block = begin + step
            at = (pos + step) * BLOCK
            spots = [(inner * span + blocks - block) * sub for inner in range(BLOCK)]
            sigmas = volatility(shard, offset, block, limit)
            rates = [rate[pl.ds(shard * state_rows + spot, 2 * sub)] for spot in spots]
            olds = [disc[pl.ds(spot, 2 * sub)] for spot in spots]
            kept = []
            for inner in range(BLOCK):
                row = block * BLOCK + inner
                sigma = sigmas[inner]
                lead = sigma * table(0, row)
                half = sigma * table(1, row)
                drive = lead - lead * olds[inner]
                sums[0] = sums[0] + drive
                tilt = sums[0]
                for f in range(1, factors):
                    scale = table(1 + f, row)
                    sums[f] = sums[f] + scale * drive
                    tilt = tilt + scale * sums[f]
                tilt = tilt - half
                new = rates[inner] * jnp.exp2((timer * lead) * tilt)
                fresh = 1.0 / (1.0 + new)
                alive = sigma > 0.0
                shown = jnp.where(alive, fresh, 1.0)
                kept.append((new, fresh, shown, tilt - half, total))
                bond = bond * shown
                total = total + jnp.where(alive, bond, 0.0)
            for inner, (new, fresh, shown, lean, before) in enumerate(kept):
                rate[pl.ds(shard * state_rows + spots[inner], 2 * sub)] = new
                disc[pl.ds(spots[inner], 2 * sub)] = fresh
                res_old[at + inner] = olds[inner]
                res_disc[at + inner] = shown
                res_tilt[at + inner] = lean
                res_sum[at + inner] = before
            return (tuple(sums), bond, total)

        steps = blocks - begin + 1
        _, bond, total = lax.fori_loop(
            0, steps, one_block, (sums, jnp.ones(pair_tile, f32), jnp.zeros(pair_tile, f32))
        )
        slot = slot_of(shard, offset)
        annuities[pl.ds(slot, 2 * sub)] = ACCRUAL * total
        finals[pl.ds(slot, 2 * sub)] = bond
        near = jnp.maximum(opening - 2, 0)
        numer = numer * (1.0 + state(rate, opening - 1, shard))
        numer = numer * jnp.where(date == 0, 1.0, 1.0 + state(rate, near, shard))
        numers[pl.ds(slot, sub)] = numer
        later = numer * (1.0 + state(rate, opening, shard)) * (
            1.0 + state(rate, opening + 1, shard)
        )
        if odd:
            later = jnp.where(offset + 1 < per_shard, later, numer)
        numers[pl.ds(slot + sub, sub)] = later
        near_fix[pl.ds(slot, sub)] = 1.0 - state(disc, near)
        last_fix[pl.ds(slot, sub)] = 1.0 - state(disc, opening - 1)
        near_fix[pl.ds(slot + sub, sub)] = 1.0 - state(disc, opening)
        last_fix[pl.ds(slot + sub, sub)] = 1.0 - state(disc, opening + 1)
        return (pos + steps, later)

    pos = jnp.int32(0)
    ends = []
    for shard in range(shards):

        for row in range(lowest[shard], forwards):
            if shard == 0:
                start = jnp.full(tile, ACCRUAL * curve_ref[row], f32)
            else:
                start = ACCRUAL * mail(shard - 1, lay.rates + row - lay.low_row)
            rate[pl.ds(shard * state_rows + place_of(row), sub)] = start
            disc[pl.ds(place_of(row), sub)] = 1.0 / (1.0 + start)
        numer = jnp.ones(tile, f32) if shard == 0 else mail(shard - 1, lay.numer)
        pos, numer = lax.fori_loop(
            0, pairs, functools.partial(forward_pair, shard), (pos, numer)
        )
        ends.append(numer)

    value = jnp.zeros(tile, f32)
    for shard in range(shards):

        def stage(index, _, shard=shard):
            offset = 2 * index
            slot = slot_of(shard, offset)
            pair = pl.ds(slot, 2 * sub)
            annuity = annuities[pair]
            floating = 1.0 - finals[pair]
            marks = []
            for step in range(2):
                spot = jnp.minimum(offset + step, per_shard - 1)
                named = smalls[(shard * lay.small_rows + lay.slot_at) * LANES + spot]
                named = named.astype(jnp.int32)
                owner = lax.div(named, per_shard)
                base = (owner * lay.small_rows + lay.regress_at) * LANES
                base = base + lax.rem(named, per_shard)
                marks.append([smalls[base + q * LANES] for q in range(basis)])
            w = [both(marks[0][q], marks[1][q]) for q in range(basis)]
            if odd:
                real = is_low | (offset + 1 < per_shard)
                annuity = jnp.where(real, annuity, 1.0)
            inverse = 1.0 / annuity
            swap = floating * inverse
            money = (swap - STRIKE) * (1.0 / SMOOTHING)
            exercise = floating - STRIKE * annuity
            inner = w[3] + money * (w[4] + money * w[5])
            continuation = w[0] + money * (w[1] + money * w[2]) + annuity * inner
            sigmoid = jax.nn.sigmoid((exercise - continuation) * (1.0 / SMOOTHING))
            flag = mail(shard, lay.flag + offset, 2)
            if odd:
                flag = jnp.where(real, flag, 0.0)
            chance = flag * sigmoid
            slope = chance * (1.0 - sigmoid) * (1.0 / SMOOTHING)
            money_adj = (
                w[1] + 2.0 * (w[2] * money) + annuity * (w[4] + 2.0 * (w[5] * money))
            ) * (1.0 / SMOOTHING)
            tilt_money = money_adj * inverse
            annuity_seed[pair] = slope * (-STRIKE - inner + tilt_money * swap)
            float_seed[pair] = slope * (1.0 - tilt_money)
            chances[pair] = chance
            pays[pair] = NOTIONAL * exercise / numers[pair]
            return 0

        lax.fori_loop(0, pairs, stage, 0, unroll=pairs)
        survive = jnp.ones(tile, f32) if shard == 0 else mail(shard - 1, lay.survive)

        def gain(offset, carry, shard=shard):
            survive, value = carry
            here = pl.ds(slot_of(shard, offset), sub)
            chance = chances[here]
            survs[here] = survive
            return (survive * (1.0 - chance), value + survive * chance * pays[here])

        survive, value = lax.fori_loop(0, per_shard, gain, (survive, value), unroll=per_shard)
    value_ref[...] = value

    late = jnp.zeros(tile, f32)
    log_adj = jnp.zeros(tile, f32)
    for shard in reversed(range(shards)):

        def unwind(step, carry, shard=shard):
            late, log_adj = carry
            here = pl.ds(slot_of(shard, per_shard - 1 - step), sub)
            chance = chances[here]
            pay = pays[here]
            survive = survs[here]
            chance_adj = survive * (pay - late)
            direct = (NOTIONAL * survive) * chance / numers[here]
            annuity_adj = chance_adj * annuity_seed[here] - STRIKE * direct
            float_adj = chance_adj * float_seed[here] + direct
            level_seed[here] = annuity_adj * annuities[here] - float_adj * finals[here]
            slope_seed[here] = ACCRUAL * annuity_adj
            gained = chance * pay
            log_adj = log_adj - survive * gained
            numer_adj[here] = log_adj
            return (gained + late * (1.0 - chance), log_adj)

        late, log_adj = lax.fori_loop(0, per_shard, unwind, (late, log_adj), unroll=per_shard)
        if odd:
            here = pl.ds(slot_of(shard, per_shard), sub)
            level_seed[here] = jnp.zeros(tile, f32)
            slope_seed[here] = jnp.zeros(tile, f32)
        if shard > 0:
            log_adj = log_adj * ends[shard - 1] / mail(shard - 1, lay.numer)

    def backward_pair(shard, back, pos):
        index = pairs - 1 - back
        offset = 2 * index
        date = shard * per_shard + offset
        opening, second = opening_pair(shard, offset)
        limit = both(opening, second)
        begin = opening // BLOCK
        horizon = horizons(date)
        slot = slot_of(shard, offset)
        level = level_seed[pl.ds(slot, 2 * sub)]
        slope = slope_seed[pl.ds(slot, 2 * sub)]
        steps = blocks - begin + 1
        first = pos - steps
        bank = (shard * pairs + index) * (blocks + 1)

        def one_block(turn, sums):
            sums = list(sums)
            step = steps - 1 - turn
            block = begin + step
            at = (first + step) * BLOCK
            spots = [(inner * span + blocks - block) * sub for inner in range(BLOCK)]
            sigmas = volatility(shard, offset, block, limit)
            laters = [adjoint[pl.ds(spot, 2 * sub)] for spot in spots]
            kept = []
            for inner in reversed(range(BLOCK)):
                row = block * BLOCK + inner
                lead = sigmas[inner] * table(0, row)
                old = res_old[at + inner]
                pull = (level - slope * res_sum[at + inner]) * (1.0 - res_disc[at + inner])
                inward = laters[inner] - pull
                timed = (horizon * lead) * inward
                sums[0] = sums[0] + timed
                drive_adj = sums[0]
                for f in range(1, factors):
                    scale = table(1 + f, row)
                    sums[f] = sums[f] + scale * timed
                    drive_adj = drive_adj + scale * sums[f]
                drive_adj = lead * drive_adj
                part = drive_adj * old
                kept.append(
                    (
                        inner,
                        inward + (part - part * old),
                        timed * res_tilt[at + inner] + (drive_adj - part),
                    )
                )
            for inner, earlier, grad in kept:
                adjoint[pl.ds(spots[inner], 2 * sub)] = earlier
                grads[
                    pl.ds(pl.multiple_of(((bank + block) * BLOCK + inner) * 2 * sub, 2 * sub), 2 * sub)
                ] = grad
            return tuple(sums)

        def patch(row, slot, fix):
            adjoint[pl.ds(place_of(row), sub)] = numer_adj[pl.ds(slot, sub)] * fix[pl.ds(slot, sub)]

        sums = (jnp.zeros(pair_tile, f32),) * factors
        turn = steps - 1 - ((opening + 1) // BLOCK - begin)
        sums = lax.fori_loop(0, turn, one_block, sums)

        def patch_second():
            patch(opening, slot + sub, near_fix)
            patch(opening + 1, slot + sub, last_fix)

        if odd:
            pl.when(offset + 1 < per_shard)(patch_second)
        else:
            patch_second()
        lax.fori_loop(turn, steps, one_block, sums)
        patch(jnp.maximum(opening - 2, 0), slot, near_fix)
        patch(opening - 1, slot, last_fix)
        return first

    for shard in reversed(range(shards)):
        pos = lax.fori_loop(0, pairs, functools.partial(backward_pair, shard), pos)
        if shard > 0:

            for row in range(lowest[shard], forwards):
                start = ACCRUAL * mail(shard - 1, lay.rates + row - lay.low_row)
                here = pl.ds(place_of(row), sub)
                adjoint[here] = adjoint[here] * state(rate, row, shard - 1) / start

    ones = jnp.ones((LANES, LANES), jnp.bfloat16)
    rows = forwards + BLOCK
    on_diagonal = lax.broadcasted_iota(jnp.int32, (rows, LANES), 0) == lax.broadcasted_iota(
        jnp.int32, (rows, LANES), 1
    )

    def along(picked):
        return jnp.dot(picked, ones, preferred_element_type=f32)

    def collect(pair, _):
        base = pair * (rows * 2 * sub)
        for half in range(2):
            picked = grads[pl.ds(base + half * sub, rows, stride=2 * sub)]
            for q in range(1, sub):
                picked = picked + grads[pl.ds(base + half * sub + q, rows, stride=2 * sub)]
            top = picked.astype(jnp.bfloat16)
            rest = (picked - top.astype(f32)).astype(jnp.bfloat16)
            total = jnp.where(on_diagonal, along(top) + along(rest), 0.0)
            line = jnp.sum(total, axis=0, keepdims=True)
            vega_ref[pl.ds(2 * pair + half, 1)] = line[:, half * BLOCK : half * BLOCK + forwards]
        return 0

    lax.fori_loop(0, shards * pairs, collect, 0, unroll=2)


def by_source(own, received, place):
    count = len(received) + 1
    parts = [own] + received[::-1]
    doubled = jnp.concatenate(parts + parts, axis=0)
    start = lax.rem(count - place, count) * own.shape[0]
    return lax.dynamic_slice_in_dim(doubled, start, count * own.shape[0], 0)


def shifted(value, axis, step):
    count = lax.axis_size(axis)
    return lax.ppermute(value, axis, [(s, (s + step) % count) for s in range(count)])


def total_over(value, axis):
    count = lax.axis_size(axis)
    if count & (count - 1):
        return lax.psum(value, axis)
    step = 1
    while step < count:
        masks = [step]
        if step > 1 and 2 * step < count:
            masks = [step, 2 * step, 3 * step]
        heard = [lax.ppermute(value, axis, [(s, s ^ mask) for s in range(count)]) for mask in masks]
        value = value + heard[0]
        if len(heard) > 1:
            value = value + (heard[1] + heard[2])
        step *= 2 if len(masks) == 1 else 4
    return value


def local(
    start_curve,
    loadings,
    vols,
    shocks,
    exercise_bits,
    regress,
    date_slot,
    ck_rates,
    ck_numer,
    ck_survive,
):
    shards = lax.axis_size("tm")
    groups = lax.axis_size("paths")
    place = lax.axis_index("tm")
    per_shard, forwards = vols.shape
    factors, paths = shocks.shape[1:]
    lay = Layout(shards, per_shard, forwards, factors, regress.shape[1], paths)
    sub, blocks, pairs = lay.sub, lay.blocks, lay.pairs
    f32 = jnp.float32
    smem = pl.BlockSpec(memory_space=pltpu.SMEM)
    vmem = pl.BlockSpec(memory_space=pltpu.VMEM)
    spot = place.reshape(1).astype(jnp.int32)

    sources = (
        shocks,
        exercise_bits,
        ck_rates,
        ck_numer,
        ck_survive,
        vols,
        regress.T,
        date_slot.reshape(1, per_shard),
    )
    sources = tuple(pltpu.with_memory_space_constraint(source, pltpu.HBM) for source in sources)
    messages = pl.pallas_call(
        functools.partial(pack_kernel, lay=lay, count=len(sources)),
        out_shape=[jax.ShapeDtypeStruct((lay.flat, LANES), f32)] * shards,
        in_specs=[smem] + [pl.BlockSpec(memory_space=pltpu.HBM)] * len(sources),
        out_specs=[vmem] * shards,
        scratch_shapes=[pltpu.VMEM(source.shape, source.dtype) for source in sources]
        + [pltpu.SemaphoreType.DMA((len(sources),))],
        compiler_params=pltpu.CompilerParams(vmem_limit_bytes=16 * 1024 * 1024),
        name="pack",
    )(spot, *sources)
    received = [shifted(messages[step], "tm", step) for step in range(1, shards)]

    loads = loadings / jnp.sqrt(jnp.sum(loadings * loadings, axis=0, keepdims=True))
    kinds = jnp.concatenate([loads[:1], 0.5 / loads[:1], loads[1:] / loads[:1]])
    ahead = jnp.pad(kinds, ((0, 0), (0, BLOCK)), constant_values=1.0)
    behind = jnp.pad(kinds, ((0, 0), (BLOCK, 0)), constant_values=1.0)
    tables = jnp.broadcast_to(
        jnp.stack([ahead, behind], axis=-1).reshape(-1, 2, 1, 1),
        (kinds.shape[0] * (forwards + BLOCK), 2, sub, LANES),
    ).reshape(-1, 2 * sub, LANES)

    iterations = sum(
        blocks - (2 * (s * per_shard + 2 * k) + 1) // BLOCK + 1
        for s in range(shards)
        for k in range(pairs)
    )
    residual = pltpu.VMEM((iterations * BLOCK, 2 * sub, LANES), f32)
    per_slot = pltpu.VMEM((shards * 2 * pairs * sub, LANES), f32)
    state_rows = BLOCK * (blocks + 2) * sub
    vega_part, value_part = pl.pallas_call(
        functools.partial(sweep_kernel, lay=lay),
        out_shape=(
            jax.ShapeDtypeStruct((shards * 2 * pairs, forwards), f32),
            jax.ShapeDtypeStruct((sub, LANES), f32),
        ),
        in_specs=[smem, smem, vmem] + [pl.BlockSpec(memory_space=pl.ANY)] * shards,
        out_specs=(vmem, vmem),
        scratch_shapes=[
            pltpu.VMEM((shards, lay.flat, LANES), f32),
            pltpu.SMEM((shards * lay.small_rows * LANES,), f32),
            pltpu.VMEM((shards * state_rows, LANES), f32),
            pltpu.VMEM((state_rows, LANES), f32),
            residual,
            residual,
            residual,
            residual,
            pltpu.VMEM((shards * pairs * (blocks + 1) * BLOCK * 2 * sub, LANES), f32),
        ]
        + [per_slot] * 13
        + [
            pltpu.VMEM((state_rows, LANES), f32),
            pltpu.SemaphoreType.DMA((shards,)),
            pltpu.SemaphoreType.DMA((shards, lay.small_rows)),
        ],
        compiler_params=pltpu.CompilerParams(vmem_limit_bytes=48 * 1024 * 1024),
        name="sweep",
    )(spot, start_curve, tables, messages[0], *received)

    parts = vega_part.reshape(shards, 2 * pairs, forwards)[:, :per_shard].reshape(shards, -1)
    cut = per_shard * forwards
    tail = jnp.broadcast_to(value_part.reshape(1, -1), (shards, lay.per_device))
    message = jnp.concatenate([parts, tail], axis=1)
    mine = lax.dynamic_index_in_dim(message, place, 0, keepdims=False)
    others = []
    for step in range(1, shards):
        sent = lax.dynamic_index_in_dim(message, lax.rem(place + step, shards), 0, keepdims=False)
        others.append(shifted(sent, "tm", step))
    path_value = by_source(
        mine[cut:].reshape(1, -1), [part[cut:].reshape(1, -1) for part in others], place
    ).reshape(-1)
    summed = mine[:cut]
    for part in others:
        summed = summed + part[:cut]
    summed = total_over(summed.reshape(per_shard, forwards), "paths")
    date = place * per_shard + jnp.arange(per_shard, dtype=jnp.int32)
    alive = jnp.arange(forwards, dtype=jnp.int32)[None, :] >= 2 * date[:, None] + 1
    weight = NOTIONAL / (paths * groups)
    vega = jnp.where(alive, summed * (weight / vols), 0.0)
    return (vega, path_value)


def solution(mesh):
    return jax.shard_map(
        local,
        mesh=mesh,
        in_specs=(
            P(),
            P(),
            P("tm", None),
            P("tm", None, "paths"),
            P("tm", "paths"),
            P("tm", None),
            P("tm"),
            P("tm", None, "paths"),
            P("tm", "paths"),
            P("tm", "paths"),
        ),
        out_specs=(P("tm", None), P("paths")),
        check_vma=False,
    )
```

time: 769 us -> 68.4 us (0.09)
  waiting for transfers between devices: 500 us -> 19.9 us
  matrix products: 103 us -> 0 us
  other arithmetic: 46.5 us -> 2.12 us
  blocking collectives: 37.9 us -> 0 us
  local copies, waits for them, and re-layouts: 34.9 us -> 2.4 us
  Pallas kernels: 0 us -> 24.9 us
  loops' own time: 13.7 us -> 0 us
  starting transfers between devices: 27.4 us -> 18 us
    ppermute x15 -> x10, waiting for transfers between devices: 500 us -> 19.9 us  [the longest x6 16.6 us: shifted(): lax.ppermute(value, axis, [(s, (s + step) % count) for s in range(count)])]
    dot_general x61 -> x0, matrix products: 103 us -> none  [the longest x20 37.6 us: segment(): jnp.einsum('ij,fjp->fip', triangle, factor_loads[:, :, None] * scaled[Non...]
    pallas_call x0 -> x2, Pallas kernels: none -> 24.9 us  [the longest x1 23.4 us: local(): pl.pallas_call(functools.partial(sweep_kernel, lay=lay), out_shape=(jax.S...]
    psum x2 -> x0, blocking collectives: 22 us -> none  [the longest x1 12.8 us: local(): vega = lax.psum(vega_part, 'paths')]
    mul x62 -> x0, other arithmetic: 16.1 us -> none  [the longest x10 6.35 us: segment(): annuity * moneyness * moneyness]
    all_gather x1 -> x0, blocking collectives: 16 us -> none  [local(): table = lax.all_gather(regress, 'tm', axis=0, tiled=True)]
    another operation x35 -> x3, local copies, waits for them, and re-layouts: 13.9 us -> 0.24 us  [the longest x2 0.16 us: local(): jnp.stack([ahead, behind], axis=-1).reshape(-1, 2, 1, 1)]
    another operation x5 -> x0, loops' own time: 13.7 us -> none  [the longest x4 12.2 us: take_turn(): lax.cond(active, do_pullback, do_nothing, incoming)]
  transfers between devices with their start and end apart: 15 -> 10, of which waited for: 8 -> 9; matrix products, arithmetic and copies ran while one was open for 2% -> 4% of each run, Pallas kernels for 0% -> 0%
where the time goes in v3:
time: 68.4 us; the launch traced here: 68.2 us
  Pallas kernels  24.9 us (36%)
  waiting for transfers between devices  19.9 us (29%)
  starting transfers between devices  18 us (26%)
  local copies, waits for them, and re-layouts  2.4 us (4%)
  other arithmetic  2.12 us (3%)
  between operations  0.81 us (1%)
    pallas_call x1, Pallas kernels, local(): pl.pallas_call(functools.partial(sweep_kernel, lay=lay), out_shape=(jax.S...  23.4 us
    ppermute x6, waiting for transfers between devices, shifted(): lax.ppermute(value, axis, [(s, (s + step) % count) for s in range(count)])  16.6 us
    ppermute x6, starting transfers between devices, shifted(): lax.ppermute(value, axis, [(s, (s + step) % count) for s in range(count)])  14.4 us
    ppermute x4, starting transfers between devices, total_over(): lax.ppermute(value, axis, [(s, s ^ mask) for s in range(count)])  3.56 us
    ppermute x4, waiting for transfers between devices, total_over(): lax.ppermute(value, axis, [(s, s ^ mask) for s in range(count)])  3.3 us
    pallas_call x1, Pallas kernels, local(): pl.pallas_call(functools.partial(pack_kernel, lay=lay, count=len(sources)...  1.54 us
  transfers between devices with their start and end apart: 10, of which 9 were waited for; matrix products, arithmetic and copies ran while one was open for 4% of the time, Pallas kernels for 0%

profile of v3, /device:TPU:0, one launch (start us, length us, event | category | flops | bytes accessed | tf_op | source)
XLA Modules:
  0.0 68.2 jit_solution(2731087275724315624)
XLA Ops:
  0.6 1.5 %pack.1 = (f32[480,128]{1,0:T(8,128)S(1)}, f32[480,128]{1,0:T(8,128)S(1)}, f32[480,128]{1,0:T(8,128)S(1)}, f32[480,128]{1,0:T(8,128)S(1)}) custom-call(s32[1]{0:T(128)} %bitcast.place_ref, f32[10,4,2048]{2,1,0:T(4,128)} %refs_0_.1, s32[10,2048]{1,0:T(8,128)} %refs_1_.1, f32[1,80,2048]{2,1,0:T(8,128)} %refs_2_.1, f32[1,2048]{1,0:T(1,128)} %refs_3_.1, ...), custom_call_target="tpu_custom_call" | custom-call | tf_op jit(solution)/shard_map/pack/pallas_call | solution.py:561
  2.2 3.1 %collective-permute-start = (f32[480,128]{1,0:T(8,128)S(1)}, f32[480,128]{1,0:T(8,128)S(1)}, u32[]{:S(2)}, u32[]{:S(2)}) collective-permute-start(f32[480,128]{1,0:T(8,128)S(1)} %get-tuple-element.9), channel_id=1, source_target_pairs={{0,8},{8,16},{16,24},{24,0},{1,9},{9,17},{17,25},{25,1},{2,10},{10... | collective-permute-start | bytes 737288 | tf_op jit(solution)/shard_map/ppermute | solution.py:506
  5.3 2.6 %collective-permute-start.1 = (f32[480,128]{1,0:T(8,128)S(1)}, f32[480,128]{1,0:T(8,128)S(1)}, u32[]{:S(2)}, u32[]{:S(2)}) collective-permute-start(f32[480,128]{1,0:T(8,128)S(1)} %get-tuple-element.10), channel_id=1, source_target_pairs={{0,16},{8,24},{16,0},{24,8},{1,17},{9,25},{17,1},{25,9},{2,18},{10... | collective-permute-start | bytes 737288 | tf_op jit(solution)/shard_map/ppermute | solution.py:506
  7.9 1.3 %collective-permute-start.2 = (f32[480,128]{1,0:T(8,128)S(1)}, f32[480,128]{1,0:T(8,128)S(1)}, u32[]{:S(2)}, u32[]{:S(2)}) collective-permute-start(f32[480,128]{1,0:T(8,128)S(1)} %get-tuple-element.11), channel_id=1, source_target_pairs={{0,24},{8,0},{16,8},{24,16},{1,25},{9,1},{17,9},{25,17},{2,26},{10... | collective-permute-start | bytes 737288 | tf_op jit(solution)/shard_map/ppermute | solution.py:506
  9.2 0.7 %multiply_reduce_fusion = f32[80]{0:T(128)S(1)} fusion(f32[4,80]{1,0:T(4,128)} %param.11), kind=kLoop, calls=%fused_computation.13 | loop fusion | flops 560 | bytes 1600 | tf_op jit(solution)/shard_map/reduce_sum | solution.py:573
  9.9 0.7 %broadcast_divide_fusion = f32[4,80]{1,0:T(4,128)S(1)} fusion(f32[4,80]{1,0:T(4,128)} %param.11, f32[80]{0:T(128)S(1)} %sqrt.8), kind=kLoop, calls=%fused_computation.14 | loop fusion | flops 320 | bytes 2880 | tf_op jit(solution)/shard_map/div | solution.py:573
  11.1 3.1 %collective-permute-done.refs_1_ = f32[480,128]{1,0:T(8,128)S(1)} collective-permute-done((f32[480,128]{1,0:T(8,128)S(1)}, f32[480,128]{1,0:T(8,128)S(1)}, u32[]{:S(2)}, u32[]{:S(2)}) %collective-permute-start) | collective-permute-done | bytes 245792 | tf_op jit(solution)/shard_map/ppermute | solution.py:506
  14.3 9.7 %collective-permute-done.1.refs_2_ = f32[480,128]{1,0:T(8,128)S(1)} collective-permute-done((f32[480,128]{1,0:T(8,128)S(1)}, f32[480,128]{1,0:T(8,128)S(1)}, u32[]{:S(2)}, u32[]{:S(2)}) %collective-permute-start.1) | collective-permute-done | bytes 245792 | tf_op jit(solution)/shard_map/ppermute | solution.py:506
  24.0 0.5 broadcast_in_dim.28.table_ref
  24.5 23.4 %sweep.1 = (f32[40,80]{1,0:T(8,128)S(1)}, f32[4,128]{1,0:T(4,128)S(1)}) custom-call(s32[1]{0:T(128)} %bitcast.place_ref, f32[80]{0:T(128)S(1)} %copy-done, f32[440,8,128]{2,1,0:T(8,128)S(1)} %broadcast_in_dim.28.table_ref, f32[480,128]{1,0:T(8,128)S(1)} %get-tuple-element.8.refs_0_, f32[480,128]{1,0:T(8,128)S(1)} %collective-permute-done.refs_1_, ...), custom_call_target="tpu_custom_call" | custom-call | tf_op jit(solution)/shard_map/sweep/pallas_call | solution.py:590
  48.1 5.8 %collective-permute-start.3 = (f32[1312]{0:T(1024)S(1)}, f32[1312]{0:T(1024)S(1)}, u32[]{:S(2)}, u32[]{:S(2)}) collective-permute-start(f32[1312]{0:T(1024)S(1)} %get-tuple-element.14), channel_id=1, source_target_pairs={{0,8},{8,16},{16,24},{24,0},{1,9},{9,17},{17,25},{25,1},{2,10},{10... | collective-permute-start | bytes 15752 | tf_op jit(solution)/shard_map/ppermute | solution.py:506
  53.9 1.1 %collective-permute-start.5 = (f32[1312]{0:T(1024)S(1)}, f32[1312]{0:T(1024)S(1)}, u32[]{:S(2)}, u32[]{:S(2)}) collective-permute-start(f32[1312]{0:T(1024)S(1)} %get-tuple-element.15), channel_id=1, source_target_pairs={{0,24},{8,0},{16,8},{24,16},{1,25},{9,1},{17,9},{25,17},{2,26},{10... | collective-permute-start | bytes 15752 | tf_op jit(solution)/shard_map/ppermute | solution.py:506
  55.0 0.5 collective-permute-start.4
  55.6 1.0 %collective-permute-done.3 = f32[1312]{0:T(1024)S(1)} collective-permute-done((f32[1312]{0:T(1024)S(1)}, f32[1312]{0:T(1024)S(1)}, u32[]{:S(2)}, u32[]{:S(2)}) %collective-permute-start.3) | collective-permute-done | bytes 5280 | tf_op jit(solution)/shard_map/ppermute | solution.py:506
  56.7 0.9 %collective-permute-done.5 = f32[1312]{0:T(1024)S(1)} collective-permute-done((f32[1312]{0:T(1024)S(1)}, f32[1312]{0:T(1024)S(1)}, u32[]{:S(2)}, u32[]{:S(2)}) %collective-permute-start.5) | collective-permute-done | bytes 5280 | tf_op jit(solution)/shard_map/ppermute | solution.py:506
  57.7 1.9 %collective-permute-done.4 = f32[1312]{0:T(1024)S(1)} collective-permute-done((f32[1312]{0:T(1024)S(1)}, f32[1312]{0:T(1024)S(1)}, u32[]{:S(2)}, u32[]{:S(2)}) %collective-permute-start.4) | collective-permute-done | bytes 5280 | tf_op jit(solution)/shard_map/ppermute | solution.py:506
  60.1 0.8 %collective-permute-done.6 = f32[10,80]{1,0:T(8,128)S(1)} collective-permute-done((f32[10,80]{1,0:T(8,128)S(1)}, f32[10,80]{1,0:T(8,128)S(1)}, u32[]{:S(2)}, u32[]{:S(2)}) %collective-permute-start.6) | collective-permute-done | bytes 3232 | tf_op jit(solution)/shard_map/ppermute | solution.py:518
  60.9 2.4 %collective-permute-start.9 = (f32[10,80]{1,0:T(8,128)S(1)}, f32[10,80]{1,0:T(8,128)S(1)}, u32[]{:S(2)}, u32[]{:S(2)}) collective-permute-start(f32[10,80]{1,0:T(8,128)S(1)} %add.84), channel_id=1, source_target_pairs={{0,6},{1,7},{2,4},{3,5},{4,2},{5,3},{6,0},{7,1},{8,14},{9,15},{10,... | collective-permute-start | bytes 9608 | tf_op jit(solution)/shard_map/ppermute | solution.py:518
  63.3 0.5 collective-permute-start.8
  63.9 0.5 collective-permute-start.7
  64.4 0.6 copy.15
  65.4 1.5 %collective-permute-done.8 = f32[10,80]{1,0:T(8,128)S(1)} collective-permute-done((f32[10,80]{1,0:T(8,128)S(1)}, f32[10,80]{1,0:T(8,128)S(1)}, u32[]{:S(2)}, u32[]{:S(2)}) %collective-permute-start.8) | collective-permute-done | bytes 3232 | tf_op jit(solution)/shard_map/ppermute | solution.py:518
  67.0 0.5 collective-permute-done.7
  67.5 0.7 multiply_select_fusion
  (40 shorter events, 1.9 us)
Async XLA Ops:
  0.6 23.8 %copy-start = (f32[80]{0:T(128)S(1)}, f32[80]{0:T(128)}, u32[]{:S(2)}) copy-start(f32[80]{0:T(128)} %curve_ref.1) | copy-start | bytes 964
  2.2 12.1 %collective-permute-start = (f32[480,128]{1,0:T(8,128)S(1)}, f32[480,128]{1,0:T(8,128)S(1)}, u32[]{:S(2)}, u32[]{:S(2)}) collective-permute-start(f32[480,128]{1,0:T(8,128)S(1)} %get-tuple-element.9), channel_id=1, source_target_pairs={{0,8},{8,16},{16,24},{24,0},{1,9},{9,17},{17,25},{25,1},{2,10},{10... | collective-permute-start | bytes 737288 | tf_op jit(solution)/shard_map/ppermute | solution.py:506
  5.3 18.6 %collective-permute-start.1 = (f32[480,128]{1,0:T(8,128)S(1)}, f32[480,128]{1,0:T(8,128)S(1)}, u32[]{:S(2)}, u32[]{:S(2)}) collective-permute-start(f32[480,128]{1,0:T(8,128)S(1)} %get-tuple-element.10), channel_id=1, source_target_pairs={{0,16},{8,24},{16,0},{24,8},{1,17},{9,25},{17,1},{25,9},{2,18},{10... | collective-permute-start | bytes 737288 | tf_op jit(solution)/shard_map/ppermute | solution.py:506
  7.9 16.1 %collective-permute-start.2 = (f32[480,128]{1,0:T(8,128)S(1)}, f32[480,128]{1,0:T(8,128)S(1)}, u32[]{:S(2)}, u32[]{:S(2)}) collective-permute-start(f32[480,128]{1,0:T(8,128)S(1)} %get-tuple-element.11), channel_id=1, source_target_pairs={{0,24},{8,0},{16,8},{24,16},{1,25},{9,1},{17,9},{25,17},{2,26},{10... | collective-permute-start | bytes 737288 | tf_op jit(solution)/shard_map/ppermute | solution.py:506
  24.5 43.0 %copy-start.1 = (f32[10,80]{1,0:T(8,128)S(1)}, f32[10,80]{1,0:T(8,128)}, u32[]{:S(2)}) copy-start(f32[10,80]{1,0:T(8,128)} %refs_5_.1) | copy-start | bytes 9604
  48.1 8.4 %collective-permute-start.3 = (f32[1312]{0:T(1024)S(1)}, f32[1312]{0:T(1024)S(1)}, u32[]{:S(2)}, u32[]{:S(2)}) collective-permute-start(f32[1312]{0:T(1024)S(1)} %get-tuple-element.14), channel_id=1, source_target_pairs={{0,8},{8,16},{16,24},{24,0},{1,9},{9,17},{17,25},{25,1},{2,10},{10... | collective-permute-start | bytes 15752 | tf_op jit(solution)/shard_map/ppermute | solution.py:506
  53.9 3.7 %collective-permute-start.5 = (f32[1312]{0:T(1024)S(1)}, f32[1312]{0:T(1024)S(1)}, u32[]{:S(2)}, u32[]{:S(2)}) collective-permute-start(f32[1312]{0:T(1024)S(1)} %get-tuple-element.15), channel_id=1, source_target_pairs={{0,24},{8,0},{16,8},{24,16},{1,25},{9,1},{17,9},{25,17},{2,26},{10... | collective-permute-start | bytes 15752 | tf_op jit(solution)/shard_map/ppermute | solution.py:506
  55.0 4.5 %collective-permute-start.4 = (f32[1312]{0:T(1024)S(1)}, f32[1312]{0:T(1024)S(1)}, u32[]{:S(2)}, u32[]{:S(2)}) collective-permute-start(f32[1312]{0:T(1024)S(1)} %get-tuple-element.16), channel_id=1, source_target_pairs={{0,16},{8,24},{16,0},{24,8},{1,17},{9,25},{17,1},{25,9},{2,18},{10... | collective-permute-start | bytes 15752 | tf_op jit(solution)/shard_map/ppermute | solution.py:506
  59.7 1.2 %collective-permute-start.6 = (f32[10,80]{1,0:T(8,128)S(1)}, f32[10,80]{1,0:T(8,128)S(1)}, u32[]{:S(2)}, u32[]{:S(2)}) collective-permute-start(f32[10,80]{1,0:T(8,128)S(1)} %add_add_fusion), channel_id=1, source_target_pairs={{0,1},{1,0},{2,3},{3,2},{4,5},{5,4},{6,7},{7,6},{8,9},{9,8},{10,11... | collective-permute-start | bytes 9608 | tf_op jit(solution)/shard_map/ppermute | solution.py:518
  60.9 4.5 %collective-permute-start.9 = (f32[10,80]{1,0:T(8,128)S(1)}, f32[10,80]{1,0:T(8,128)S(1)}, u32[]{:S(2)}, u32[]{:S(2)}) collective-permute-start(f32[10,80]{1,0:T(8,128)S(1)} %add.84), channel_id=1, source_target_pairs={{0,6},{1,7},{2,4},{3,5},{4,2},{5,3},{6,0},{7,1},{8,14},{9,15},{10,... | collective-permute-start | bytes 9608 | tf_op jit(solution)/shard_map/ppermute | solution.py:518
  63.3 3.7 %collective-permute-start.8 = (f32[10,80]{1,0:T(8,128)S(1)}, f32[10,80]{1,0:T(8,128)S(1)}, u32[]{:S(2)}, u32[]{:S(2)}) collective-permute-start(f32[10,80]{1,0:T(8,128)S(1)} %add.84), channel_id=1, source_target_pairs={{0,4},{1,5},{2,6},{3,7},{4,0},{5,1},{6,2},{7,3},{8,12},{9,13},{10,... | collective-permute-start | bytes 9608 | tf_op jit(solution)/shard_map/ppermute | solution.py:518
  63.9 3.7 %collective-permute-start.7 = (f32[10,80]{1,0:T(8,128)S(1)}, f32[10,80]{1,0:T(8,128)S(1)}, u32[]{:S(2)}, u32[]{:S(2)}) collective-permute-start(f32[10,80]{1,0:T(8,128)S(1)} %add.84), channel_id=1, source_target_pairs={{0,2},{1,3},{2,0},{3,1},{4,6},{5,7},{6,4},{7,5},{8,10},{9,11},{10,... | collective-permute-start | bytes 9608 | tf_op jit(solution)/shard_map/ppermute | solution.py:518

commit v4 on v3

--- a/solution.py
+++ b/solution.py
@@ -96,6 +96,7 @@
         res_disc,
         res_tilt,
         res_sum,
+        res_lead,
         grads,
         annuities,
         finals,
@@ -122,7 +123,8 @@
     span = blocks + 2
     state_rows = BLOCK * span * sub
     lowest = [max(0, 2 * s * per_shard - 1) for s in range(shards)]
-    is_low = lax.broadcasted_iota(jnp.int32, pair_tile, 0) < sub
+    side = lax.broadcasted_iota(jnp.int32, pair_tile, 0)
+    is_low = side < sub
 
     def fetch(step):
         source = lax.rem(place - step + shards, shards)
@@ -187,17 +189,13 @@
             second = jnp.where(offset + 1 < per_shard, second, 4 * forwards)
         return opening, second
 
-    inner_of = [
-        both(0, BLOCK) - inner for inner in range(BLOCK)
-    ]
-
-    def volatility(shard, offset, block, limit):
+    def volatility(shard, offset, block, reach):
         base = (shard * lay.small_rows + offset) * LANES + block * BLOCK
-        first = jnp.broadcast_to(block * BLOCK, pair_tile)
+        beyond = block * BLOCK - reach
         found = []
         for inner in range(BLOCK):
             raw = both(smalls[base + inner], smalls[base + (LANES - BLOCK + inner)])
-            found.append(jnp.where(first >= limit + inner_of[inner], raw, 0.0))
+            found.append(jnp.where(beyond >= -inner, raw, 0.0))
         return found
 
     def table(kind, row):
@@ -208,7 +206,7 @@
         offset = 2 * index
         date = shard * per_shard + offset
         opening, second = opening_pair(shard, offset)
-        limit = both(opening, second)
+        reach = both(opening, second + BLOCK)
         begin = opening // BLOCK
         horizon = horizons(date)
         timer = horizon * LOG2E
@@ -226,8 +224,8 @@
             sums = list(sums)
             block = begin + step
             at = (pos + step) * BLOCK
-            spots = [(inner * span + blocks - block) * sub for inner in range(BLOCK)]
-            sigmas = volatility(shard, offset, block, limit)
+            spots = [(blocks - block) * sub + inner * (span * sub) for inner in range(BLOCK)]
+            sigmas = volatility(shard, offset, block, reach)
             rates = [rate[pl.ds(shard * state_rows + spot, 2 * sub)] for spot in spots]
             olds = [disc[pl.ds(spot, 2 * sub)] for spot in spots]
             kept = []
@@ -248,16 +246,17 @@
                 fresh = 1.0 / (1.0 + new)
                 alive = sigma > 0.0
                 shown = jnp.where(alive, fresh, 1.0)
-                kept.append((new, fresh, shown, tilt - half, total))
+                kept.append((new, fresh, shown, tilt - half, total, lead))
                 bond = bond * shown
                 total = total + jnp.where(alive, bond, 0.0)
-            for inner, (new, fresh, shown, lean, before) in enumerate(kept):
+            for inner, (new, fresh, shown, lean, before, lead) in enumerate(kept):
                 rate[pl.ds(shard * state_rows + spots[inner], 2 * sub)] = new
                 disc[pl.ds(spots[inner], 2 * sub)] = fresh
                 res_old[at + inner] = olds[inner]
                 res_disc[at + inner] = shown
                 res_tilt[at + inner] = lean
                 res_sum[at + inner] = before
+                res_lead[at + inner] = lead
             return (tuple(sums), bond, total)
 
         steps = blocks - begin + 1
@@ -390,8 +389,7 @@
         index = pairs - 1 - back
         offset = 2 * index
         date = shard * per_shard + offset
-        opening, second = opening_pair(shard, offset)
-        limit = both(opening, second)
+        opening, _ = opening_pair(shard, offset)
         begin = opening // BLOCK
         horizon = horizons(date)
         slot = slot_of(shard, offset)
@@ -406,13 +404,12 @@
             step = steps - 1 - turn
             block = begin + step
             at = (first + step) * BLOCK
-            spots = [(inner * span + blocks - block) * sub for inner in range(BLOCK)]
-            sigmas = volatility(shard, offset, block, limit)
+            spots = [(blocks - block) * sub + inner * (span * sub) for inner in range(BLOCK)]
             laters = [adjoint[pl.ds(spot, 2 * sub)] for spot in spots]
             kept = []
             for inner in reversed(range(BLOCK)):
                 row = block * BLOCK + inner
-                lead = sigmas[inner] * table(0, row)
+                lead = res_lead[at + inner]
                 old = res_old[at + inner]
                 pull = (level - slope * res_sum[at + inner]) * (1.0 - res_disc[at + inner])
                 inward = laters[inner] - pull
@@ -432,11 +429,23 @@
                         timed * res_tilt[at + inner] + (drive_adj - part),
                     )
                 )
-            for inner, earlier, grad in kept:
+            for inner, earlier, _ in kept:
                 adjoint[pl.ds(spots[inner], 2 * sub)] = earlier
-                grads[
-                    pl.ds(pl.multiple_of(((bank + block) * BLOCK + inner) * 2 * sub, 2 * sub), 2 * sub)
-                ] = grad
+            folded = [grad for _, _, grad in reversed(kept)]
+            reach = 1
+            while reach < sub:
+                kept_side = (side // reach) % 2 == 0
+                folded = [
+                    jnp.where(
+                        kept_side,
+                        first_half + pltpu.roll(first_half, 2 * sub - reach, 0),
+                        second_half + pltpu.roll(second_half, reach, 0),
+                    )
+                    for first_half, second_half in zip(folded[::2], folded[1::2])
+                ]
+                reach *= 2
+            for index, grad in enumerate(folded):
+                grads[(bank + block) * (BLOCK // sub) + index] = grad
             return tuple(sums)
 
         def patch(row, slot, fix):
@@ -469,28 +478,29 @@
                 adjoint[here] = adjoint[here] * state(rate, row, shard - 1) / start
 
     ones = jnp.ones((LANES, LANES), jnp.bfloat16)
-    rows = forwards + BLOCK
-    on_diagonal = lax.broadcasted_iota(jnp.int32, (rows, LANES), 0) == lax.broadcasted_iota(
-        jnp.int32, (rows, LANES), 1
-    )
+    pieces = (blocks + 1) * (BLOCK // sub)
+    shape = (pieces, 2 * sub, LANES)
+    spread = lax.broadcasted_iota(jnp.int32, shape, 0) * sub
+    spread = spread + lax.broadcasted_iota(jnp.int32, shape, 1)
+    spread = jnp.where(lax.broadcasted_iota(jnp.int32, shape, 1) < sub, spread, spread - sub - BLOCK)
+    on_lane = spread == lax.broadcasted_iota(jnp.int32, shape, 2)
 
     def along(picked):
         return jnp.dot(picked, ones, preferred_element_type=f32)
 
     def collect(pair, _):
-        base = pair * (rows * 2 * sub)
-        for half in range(2):
-            picked = grads[pl.ds(base + half * sub, rows, stride=2 * sub)]
-            for q in range(1, sub):
-                picked = picked + grads[pl.ds(base + half * sub + q, rows, stride=2 * sub)]
-            top = picked.astype(jnp.bfloat16)
-            rest = (picked - top.astype(f32)).astype(jnp.bfloat16)
-            total = jnp.where(on_diagonal, along(top) + along(rest), 0.0)
-            line = jnp.sum(total, axis=0, keepdims=True)
-            vega_ref[pl.ds(2 * pair + half, 1)] = line[:, half * BLOCK : half * BLOCK + forwards]
+        picked = grads[pl.ds(pair * pieces, pieces)].reshape(pieces * 2 * sub, LANES)
+        top = picked.astype(jnp.bfloat16)
+        rest = (picked - top.astype(f32)).astype(jnp.bfloat16)
+        total = jnp.where(on_lane, (along(top) + along(rest)).reshape(shape), 0.0)
+        total = jnp.sum(total, axis=0)
+        low = jnp.sum(jnp.where(is_low, total, 0.0), axis=0, keepdims=True)
+        high = jnp.sum(jnp.where(is_low, 0.0, total), axis=0, keepdims=True)
+        vega_ref[pl.ds(2 * pair, 1)] = low[:, :forwards]
+        vega_ref[pl.ds(2 * pair + 1, 1)] = high[:, :forwards]
         return 0
 
-    lax.fori_loop(0, shards * pairs, collect, 0, unroll=2)
+    lax.fori_loop(0, shards * pairs, collect, 0, unroll=4)
 
 
 def by_source(own, received, place):
@@ -604,7 +614,8 @@
             residual,
             residual,
             residual,
-            pltpu.VMEM((shards * pairs * (blocks + 1) * BLOCK * 2 * sub, LANES), f32),
+            residual,
+            pltpu.VMEM((shards * pairs * (blocks + 1) * (BLOCK // sub), 2 * sub, LANES), f32),
         ]
         + [per_slot] * 13
         + [

time: 68.4 us -> 66.2 us (0.968)
  Pallas kernels: 24.9 us -> 22.8 us
    pallas_call x1, Pallas kernels: 23.4 us -> 21.2 us  [local(): pl.pallas_call(functools.partial(sweep_kernel, lay=lay), out_shape=(jax.S...]
  transfers between devices with their start and end apart: 10 -> 10, of which waited for: 9 -> 9; matrix products, arithmetic and copies ran while one was open for 4% -> 5% of each run, Pallas kernels for 0% -> 0%
where the time goes in v4:
time: 66.2 us; the launch traced here: 66 us
  Pallas kernels  22.8 us (34%)
  waiting for transfers between devices  19.9 us (30%)
  starting transfers between devices  18 us (27%)
  local copies, waits for them, and re-layouts  2.4 us (4%)
  other arithmetic  2.12 us (3%)
  between operations  0.81 us (1%)
    pallas_call x1, Pallas kernels, local(): pl.pallas_call(functools.partial(sweep_kernel, lay=lay), out_shape=(jax.S...  21.2 us
    ppermute x6, waiting for transfers between devices, shifted(): lax.ppermute(value, axis, [(s, (s + step) % count) for s in range(count)])  16.6 us
    ppermute x6, starting transfers between devices, shifted(): lax.ppermute(value, axis, [(s, (s + step) % count) for s in range(count)])  14.4 us
    ppermute x4, starting transfers between devices, total_over(): lax.ppermute(value, axis, [(s, s ^ mask) for s in range(count)])  3.56 us
    ppermute x4, waiting for transfers between devices, total_over(): lax.ppermute(value, axis, [(s, s ^ mask) for s in range(count)])  3.3 us
    pallas_call x1, Pallas kernels, local(): pl.pallas_call(functools.partial(pack_kernel, lay=lay, count=len(sources)...  1.54 us
  transfers between devices with their start and end apart: 10, of which 9 were waited for; matrix products, arithmetic and copies ran while one was open for 5% of the time, Pallas kernels for 0%

profile of v4, /device:TPU:0, one launch (start us, length us, event | category | flops | bytes accessed | tf_op | source)
XLA Modules:
  0.0 66.0 jit_solution(5336659824044774888)
XLA Ops:
  0.6 1.5 %pack.1 = (f32[480,128]{1,0:T(8,128)S(1)}, f32[480,128]{1,0:T(8,128)S(1)}, f32[480,128]{1,0:T(8,128)S(1)}, f32[480,128]{1,0:T(8,128)S(1)}) custom-call(s32[1]{0:T(128)} %bitcast.place_ref, f32[10,4,2048]{2,1,0:T(4,128)} %refs_0_.1, s32[10,2048]{1,0:T(8,128)} %refs_1_.1, f32[1,80,2048]{2,1,0:T(8,128)} %refs_2_.1, f32[1,2048]{1,0:T(1,128)} %refs_3_.1, ...), custom_call_target="tpu_custom_call" | custom-call | tf_op jit(solution)/shard_map/pack/pallas_call | solution.py:571
  2.2 3.1 %collective-permute-start = (f32[480,128]{1,0:T(8,128)S(1)}, f32[480,128]{1,0:T(8,128)S(1)}, u32[]{:S(2)}, u32[]{:S(2)}) collective-permute-start(f32[480,128]{1,0:T(8,128)S(1)} %get-tuple-element.9), channel_id=1, source_target_pairs={{0,8},{8,16},{16,24},{24,0},{1,9},{9,17},{17,25},{25,1},{2,10},{10... | collective-permute-start | bytes 737288 | tf_op jit(solution)/shard_map/ppermute | solution.py:516
  5.3 2.6 %collective-permute-start.1 = (f32[480,128]{1,0:T(8,128)S(1)}, f32[480,128]{1,0:T(8,128)S(1)}, u32[]{:S(2)}, u32[]{:S(2)}) collective-permute-start(f32[480,128]{1,0:T(8,128)S(1)} %get-tuple-element.10), channel_id=1, source_target_pairs={{0,16},{8,24},{16,0},{24,8},{1,17},{9,25},{17,1},{25,9},{2,18},{10... | collective-permute-start | bytes 737288 | tf_op jit(solution)/shard_map/ppermute | solution.py:516
  7.9 1.3 %collective-permute-start.2 = (f32[480,128]{1,0:T(8,128)S(1)}, f32[480,128]{1,0:T(8,128)S(1)}, u32[]{:S(2)}, u32[]{:S(2)}) collective-permute-start(f32[480,128]{1,0:T(8,128)S(1)} %get-tuple-element.11), channel_id=1, source_target_pairs={{0,24},{8,0},{16,8},{24,16},{1,25},{9,1},{17,9},{25,17},{2,26},{10... | collective-permute-start | bytes 737288 | tf_op jit(solution)/shard_map/ppermute | solution.py:516
  9.2 0.7 %multiply_reduce_fusion = f32[80]{0:T(128)S(1)} fusion(f32[4,80]{1,0:T(4,128)} %param.11), kind=kLoop, calls=%fused_computation.13 | loop fusion | flops 560 | bytes 1600 | tf_op jit(solution)/shard_map/reduce_sum | solution.py:583
  9.9 0.7 %broadcast_divide_fusion = f32[4,80]{1,0:T(4,128)S(1)} fusion(f32[4,80]{1,0:T(4,128)} %param.11, f32[80]{0:T(128)S(1)} %sqrt.8), kind=kLoop, calls=%fused_computation.14 | loop fusion | flops 320 | bytes 2880 | tf_op jit(solution)/shard_map/div | solution.py:583
  11.1 3.1 %collective-permute-done.refs_1_ = f32[480,128]{1,0:T(8,128)S(1)} collective-permute-done((f32[480,128]{1,0:T(8,128)S(1)}, f32[480,128]{1,0:T(8,128)S(1)}, u32[]{:S(2)}, u32[]{:S(2)}) %collective-permute-start) | collective-permute-done | bytes 245792 | tf_op jit(solution)/shard_map/ppermute | solution.py:516
  14.3 9.7 %collective-permute-done.1.refs_2_ = f32[480,128]{1,0:T(8,128)S(1)} collective-permute-done((f32[480,128]{1,0:T(8,128)S(1)}, f32[480,128]{1,0:T(8,128)S(1)}, u32[]{:S(2)}, u32[]{:S(2)}) %collective-permute-start.1) | collective-permute-done | bytes 245792 | tf_op jit(solution)/shard_map/ppermute | solution.py:516
  24.0 0.5 broadcast_in_dim.28.table_ref
  24.5 21.2 %sweep.1 = (f32[40,80]{1,0:T(8,128)S(1)}, f32[4,128]{1,0:T(4,128)S(1)}) custom-call(s32[1]{0:T(128)} %bitcast.place_ref, f32[80]{0:T(128)S(1)} %copy-done, f32[440,8,128]{2,1,0:T(8,128)S(1)} %broadcast_in_dim.28.table_ref, f32[480,128]{1,0:T(8,128)S(1)} %get-tuple-element.8.refs_0_, f32[480,128]{1,0:T(8,128)S(1)} %collective-permute-done.refs_1_, ...), custom_call_target="tpu_custom_call" | custom-call | tf_op jit(solution)/shard_map/sweep/pallas_call | solution.py:600
  46.0 5.8 %collective-permute-start.3 = (f32[1312]{0:T(1024)S(1)}, f32[1312]{0:T(1024)S(1)}, u32[]{:S(2)}, u32[]{:S(2)}) collective-permute-start(f32[1312]{0:T(1024)S(1)} %get-tuple-element.14), channel_id=1, source_target_pairs={{0,8},{8,16},{16,24},{24,0},{1,9},{9,17},{17,25},{25,1},{2,10},{10... | collective-permute-start | bytes 15752 | tf_op jit(solution)/shard_map/ppermute | solution.py:516
  51.8 1.1 %collective-permute-start.5 = (f32[1312]{0:T(1024)S(1)}, f32[1312]{0:T(1024)S(1)}, u32[]{:S(2)}, u32[]{:S(2)}) collective-permute-start(f32[1312]{0:T(1024)S(1)} %get-tuple-element.15), channel_id=1, source_target_pairs={{0,24},{8,0},{16,8},{24,16},{1,25},{9,1},{17,9},{25,17},{2,26},{10... | collective-permute-start | bytes 15752 | tf_op jit(solution)/shard_map/ppermute | solution.py:516
  52.8 0.5 collective-permute-start.4
  53.4 1.0 %collective-permute-done.3 = f32[1312]{0:T(1024)S(1)} collective-permute-done((f32[1312]{0:T(1024)S(1)}, f32[1312]{0:T(1024)S(1)}, u32[]{:S(2)}, u32[]{:S(2)}) %collective-permute-start.3) | collective-permute-done | bytes 5280 | tf_op jit(solution)/shard_map/ppermute | solution.py:516
  54.5 0.9 %collective-permute-done.5 = f32[1312]{0:T(1024)S(1)} collective-permute-done((f32[1312]{0:T(1024)S(1)}, f32[1312]{0:T(1024)S(1)}, u32[]{:S(2)}, u32[]{:S(2)}) %collective-permute-start.5) | collective-permute-done | bytes 5280 | tf_op jit(solution)/shard_map/ppermute | solution.py:516
  55.5 1.9 %collective-permute-done.4 = f32[1312]{0:T(1024)S(1)} collective-permute-done((f32[1312]{0:T(1024)S(1)}, f32[1312]{0:T(1024)S(1)}, u32[]{:S(2)}, u32[]{:S(2)}) %collective-permute-start.4) | collective-permute-done | bytes 5280 | tf_op jit(solution)/shard_map/ppermute | solution.py:516
  57.9 0.8 %collective-permute-done.6 = f32[10,80]{1,0:T(8,128)S(1)} collective-permute-done((f32[10,80]{1,0:T(8,128)S(1)}, f32[10,80]{1,0:T(8,128)S(1)}, u32[]{:S(2)}, u32[]{:S(2)}) %collective-permute-start.6) | collective-permute-done | bytes 3232 | tf_op jit(solution)/shard_map/ppermute | solution.py:528
  58.7 2.4 %collective-permute-start.9 = (f32[10,80]{1,0:T(8,128)S(1)}, f32[10,80]{1,0:T(8,128)S(1)}, u32[]{:S(2)}, u32[]{:S(2)}) collective-permute-start(f32[10,80]{1,0:T(8,128)S(1)} %add.84), channel_id=1, source_target_pairs={{0,6},{1,7},{2,4},{3,5},{4,2},{5,3},{6,0},{7,1},{8,14},{9,15},{10,... | collective-permute-start | bytes 9608 | tf_op jit(solution)/shard_map/ppermute | solution.py:528
  61.2 0.5 collective-permute-start.8
  61.7 0.5 collective-permute-start.7
  62.2 0.6 copy.15
  63.3 1.5 %collective-permute-done.8 = f32[10,80]{1,0:T(8,128)S(1)} collective-permute-done((f32[10,80]{1,0:T(8,128)S(1)}, f32[10,80]{1,0:T(8,128)S(1)}, u32[]{:S(2)}, u32[]{:S(2)}) %collective-permute-start.8) | collective-permute-done | bytes 3232 | tf_op jit(solution)/shard_map/ppermute | solution.py:528
  64.8 0.5 collective-permute-done.7
  65.3 0.7 %multiply_select_fusion = f32[10,80]{1,0:T(8,128)} fusion(f32[10,80]{1,0:T(8,128)S(1)} %copy-done.1, f32[10,80]{1,0:T(8,128)S(1)} %collective-permute-done.8, f32[10,80]{1,0:T(8,128)S(1)} %collective-permute-done.9, f32[10,80]{1,0:T(8,128)S(1)} %add.84, f32[10,80]{1,0:T(8,128)S(1)} %collective-permute-done.7, s32[10]{0:T(128)S(1)} %multiply_add_fusion), kind=kLoop, calls=%fused_computation.2 | loop fusion | flops 5600 | bytes 19240 | tf_op jit(solution)/shard_map/jit(_where)/select_n | solution.py:649
  (40 shorter events, 1.9 us)
Async XLA Ops:
  0.6 23.8 %copy-start = (f32[80]{0:T(128)S(1)}, f32[80]{0:T(128)}, u32[]{:S(2)}) copy-start(f32[80]{0:T(128)} %curve_ref.1) | copy-start | bytes 964
  2.2 12.1 %collective-permute-start = (f32[480,128]{1,0:T(8,128)S(1)}, f32[480,128]{1,0:T(8,128)S(1)}, u32[]{:S(2)}, u32[]{:S(2)}) collective-permute-start(f32[480,128]{1,0:T(8,128)S(1)} %get-tuple-element.9), channel_id=1, source_target_pairs={{0,8},{8,16},{16,24},{24,0},{1,9},{9,17},{17,25},{25,1},{2,10},{10... | collective-permute-start | bytes 737288 | tf_op jit(solution)/shard_map/ppermute | solution.py:516
  5.3 18.6 %collective-permute-start.1 = (f32[480,128]{1,0:T(8,128)S(1)}, f32[480,128]{1,0:T(8,128)S(1)}, u32[]{:S(2)}, u32[]{:S(2)}) collective-permute-start(f32[480,128]{1,0:T(8,128)S(1)} %get-tuple-element.10), channel_id=1, source_target_pairs={{0,16},{8,24},{16,0},{24,8},{1,17},{9,25},{17,1},{25,9},{2,18},{10... | collective-permute-start | bytes 737288 | tf_op jit(solution)/shard_map/ppermute | solution.py:516
  7.9 16.1 %collective-permute-start.2 = (f32[480,128]{1,0:T(8,128)S(1)}, f32[480,128]{1,0:T(8,128)S(1)}, u32[]{:S(2)}, u32[]{:S(2)}) collective-permute-start(f32[480,128]{1,0:T(8,128)S(1)} %get-tuple-element.11), channel_id=1, source_target_pairs={{0,24},{8,0},{16,8},{24,16},{1,25},{9,1},{17,9},{25,17},{2,26},{10... | collective-permute-start | bytes 737288 | tf_op jit(solution)/shard_map/ppermute | solution.py:516
  24.5 40.8 %copy-start.1 = (f32[10,80]{1,0:T(8,128)S(1)}, f32[10,80]{1,0:T(8,128)}, u32[]{:S(2)}) copy-start(f32[10,80]{1,0:T(8,128)} %refs_5_.1) | copy-start | bytes 9604
  46.0 8.4 %collective-permute-start.3 = (f32[1312]{0:T(1024)S(1)}, f32[1312]{0:T(1024)S(1)}, u32[]{:S(2)}, u32[]{:S(2)}) collective-permute-start(f32[1312]{0:T(1024)S(1)} %get-tuple-element.14), channel_id=1, source_target_pairs={{0,8},{8,16},{16,24},{24,0},{1,9},{9,17},{17,25},{25,1},{2,10},{10... | collective-permute-start | bytes 15752 | tf_op jit(solution)/shard_map/ppermute | solution.py:516
  51.8 3.7 %collective-permute-start.5 = (f32[1312]{0:T(1024)S(1)}, f32[1312]{0:T(1024)S(1)}, u32[]{:S(2)}, u32[]{:S(2)}) collective-permute-start(f32[1312]{0:T(1024)S(1)} %get-tuple-element.15), channel_id=1, source_target_pairs={{0,24},{8,0},{16,8},{24,16},{1,25},{9,1},{17,9},{25,17},{2,26},{10... | collective-permute-start | bytes 15752 | tf_op jit(solution)/shard_map/ppermute | solution.py:516
  52.8 4.5 %collective-permute-start.4 = (f32[1312]{0:T(1024)S(1)}, f32[1312]{0:T(1024)S(1)}, u32[]{:S(2)}, u32[]{:S(2)}) collective-permute-start(f32[1312]{0:T(1024)S(1)} %get-tuple-element.16), channel_id=1, source_target_pairs={{0,16},{8,24},{16,0},{24,8},{1,17},{9,25},{17,1},{25,9},{2,18},{10... | collective-permute-start | bytes 15752 | tf_op jit(solution)/shard_map/ppermute | solution.py:516
  57.5 1.2 %collective-permute-start.6 = (f32[10,80]{1,0:T(8,128)S(1)}, f32[10,80]{1,0:T(8,128)S(1)}, u32[]{:S(2)}, u32[]{:S(2)}) collective-permute-start(f32[10,80]{1,0:T(8,128)S(1)} %add_add_fusion), channel_id=1, source_target_pairs={{0,1},{1,0},{2,3},{3,2},{4,5},{5,4},{6,7},{7,6},{8,9},{9,8},{10,11... | collective-permute-start | bytes 9608 | tf_op jit(solution)/shard_map/ppermute | solution.py:528
  58.7 4.5 %collective-permute-start.9 = (f32[10,80]{1,0:T(8,128)S(1)}, f32[10,80]{1,0:T(8,128)S(1)}, u32[]{:S(2)}, u32[]{:S(2)}) collective-permute-start(f32[10,80]{1,0:T(8,128)S(1)} %add.84), channel_id=1, source_target_pairs={{0,6},{1,7},{2,4},{3,5},{4,2},{5,3},{6,0},{7,1},{8,14},{9,15},{10,... | collective-permute-start | bytes 9608 | tf_op jit(solution)/shard_map/ppermute | solution.py:528
  61.2 3.7 %collective-permute-start.8 = (f32[10,80]{1,0:T(8,128)S(1)}, f32[10,80]{1,0:T(8,128)S(1)}, u32[]{:S(2)}, u32[]{:S(2)}) collective-permute-start(f32[10,80]{1,0:T(8,128)S(1)} %add.84), channel_id=1, source_target_pairs={{0,4},{1,5},{2,6},{3,7},{4,0},{5,1},{6,2},{7,3},{8,12},{9,13},{10,... | collective-permute-start | bytes 9608 | tf_op jit(solution)/shard_map/ppermute | solution.py:528
  61.7 3.7 %collective-permute-start.7 = (f32[10,80]{1,0:T(8,128)S(1)}, f32[10,80]{1,0:T(8,128)S(1)}, u32[]{:S(2)}, u32[]{:S(2)}) collective-permute-start(f32[10,80]{1,0:T(8,128)S(1)} %add.84), channel_id=1, source_target_pairs={{0,2},{1,3},{2,0},{3,1},{4,6},{5,7},{6,4},{7,5},{8,10},{9,11},{10,... | collective-permute-start | bytes 9608 | tf_op jit(solution)/shard_map/ppermute | solution.py:528

commit v5 on v4

--- a/solution.py
+++ b/solution.py
@@ -126,23 +126,28 @@
     side = lax.broadcasted_iota(jnp.int32, pair_tile, 0)
     is_low = side < sub
 
-    def fetch(step):
-        source = lax.rem(place - step + shards, shards)
-        return pltpu.make_async_copy(block_refs[step], inbox.at[source], arrived.at[step])
-
-    def fetch_small(step, row):
-        source = lax.rem(place - step + shards, shards)
+    def fetch(step, source):
+        return pltpu.make_async_copy(block_refs[step], inbox.at[source], arrived.at[source])
+
+    def fetch_small(step, source, row):
         spot = (source * lay.small_rows + row) * LANES
         return pltpu.make_async_copy(
             block_refs[step].at[lay.small + row],
             smalls.at[pl.ds(pl.multiple_of(spot, LANES), LANES)],
-            small_arrived.at[step, row],
+            small_arrived.at[source, row],
         )
 
     for step in range(shards):
-        fetch(step).start()
+        source = lax.rem(place - step + shards, shards)
         for row in range(lay.small_rows):
-            fetch_small(step, row).start()
+            fetch_small(step, source, row).start()
+    for step in range(shards):
+        fetch(step, lax.rem(place - step + shards, shards)).start()
+
+    def await_source(shard):
+        for row in range(lay.small_rows):
+            fetch_small(0, shard, row).wait()
+        fetch(0, shard).wait()
 
     def clear(ref):
         rows = ref.shape[0]
@@ -156,11 +161,6 @@
     clear(rate)
     clear(disc)
     clear(adjoint)
-
-    for step in range(shards):
-        fetch(step).wait()
-        for row in range(lay.small_rows):
-            fetch_small(step, row).wait()
 
     def mail(shard, row, count=1):
         return inbox[shard, pl.ds(row * sub, count * sub)]
@@ -285,7 +285,7 @@
     pos = jnp.int32(0)
     ends = []
     for shard in range(shards):
-
+        await_source(shard)
         for row in range(lowest[shard], forwards):
             if shard == 0:
                 start = jnp.full(tile, ACCRUAL * curve_ref[row], f32)
@@ -578,7 +578,10 @@
         compiler_params=pltpu.CompilerParams(vmem_limit_bytes=16 * 1024 * 1024),
         name="pack",
     )(spot, *sources)
-    received = [shifted(messages[step], "tm", step) for step in range(1, shards)]
+    sent_by = {}
+    for step in reversed(range(1, shards)):
+        sent_by[step] = shifted(messages[step], "tm", step)
+    received = [sent_by[step] for step in range(1, shards)]
 
     loads = loadings / jnp.sqrt(jnp.sum(loadings * loadings, axis=0, keepdims=True))
     kinds = jnp.concatenate([loads[:1], 0.5 / loads[:1], loads[1:] / loads[:1]])

time: 66.2 us -> 66.2 us (level)
  no operation moved by 1% of the time
where the time goes in v5:
time: 66.2 us; the launch traced here: 66 us
  Pallas kernels  22.8 us (34%)
  waiting for transfers between devices  19.9 us (30%)
  starting transfers between devices  18 us (27%)
  local copies, waits for them, and re-layouts  2.4 us (4%)
  other arithmetic  2.12 us (3%)
  between operations  0.81 us (1%)
    pallas_call x1, Pallas kernels, local(): pl.pallas_call(functools.partial(sweep_kernel, lay=lay), out_shape=(jax.S...  21.2 us
    ppermute x6, waiting for transfers between devices, shifted(): lax.ppermute(value, axis, [(s, (s + step) % count) for s in range(count)])  16.6 us
    ppermute x6, starting transfers between devices, shifted(): lax.ppermute(value, axis, [(s, (s + step) % count) for s in range(count)])  14.4 us
    ppermute x4, starting transfers between devices, total_over(): lax.ppermute(value, axis, [(s, s ^ mask) for s in range(count)])  3.56 us
    ppermute x4, waiting for transfers between devices, total_over(): lax.ppermute(value, axis, [(s, s ^ mask) for s in range(count)])  3.3 us
    pallas_call x1, Pallas kernels, local(): pl.pallas_call(functools.partial(pack_kernel, lay=lay, count=len(sources)...  1.54 us
  transfers between devices with their start and end apart: 10, of which 9 were waited for; matrix products, arithmetic and copies ran while one was open for 5% of the time, Pallas kernels for 0%

profile of v5, /device:TPU:0, one launch (start us, length us, event | category | flops | bytes accessed | tf_op | source)
XLA Modules:
  0.0 66.0 jit_solution(17843119551230017412)
XLA Ops:
  0.6 1.5 %pack.1 = (f32[480,128]{1,0:T(8,128)S(1)}, f32[480,128]{1,0:T(8,128)S(1)}, f32[480,128]{1,0:T(8,128)S(1)}, f32[480,128]{1,0:T(8,128)S(1)}) custom-call(s32[1]{0:T(128)} %bitcast.place_ref, f32[10,4,2048]{2,1,0:T(4,128)} %refs_0_.1, s32[10,2048]{1,0:T(8,128)} %refs_1_.1, f32[1,80,2048]{2,1,0:T(8,128)} %refs_2_.1, f32[1,2048]{1,0:T(1,128)} %refs_3_.1, ...), custom_call_target="tpu_custom_call" | custom-call | tf_op jit(solution)/shard_map/pack/pallas_call | solution.py:571
  2.2 3.1 %collective-permute-start = (f32[480,128]{1,0:T(8,128)S(1)}, f32[480,128]{1,0:T(8,128)S(1)}, u32[]{:S(2)}, u32[]{:S(2)}) collective-permute-start(f32[480,128]{1,0:T(8,128)S(1)} %get-tuple-element.9), channel_id=1, source_target_pairs={{0,8},{8,16},{16,24},{24,0},{1,9},{9,17},{17,25},{25,1},{2,10},{10... | collective-permute-start | bytes 737288 | tf_op jit(solution)/shard_map/ppermute | solution.py:516
  5.3 2.6 %collective-permute-start.1 = (f32[480,128]{1,0:T(8,128)S(1)}, f32[480,128]{1,0:T(8,128)S(1)}, u32[]{:S(2)}, u32[]{:S(2)}) collective-permute-start(f32[480,128]{1,0:T(8,128)S(1)} %get-tuple-element.10), channel_id=1, source_target_pairs={{0,16},{8,24},{16,0},{24,8},{1,17},{9,25},{17,1},{25,9},{2,18},{10... | collective-permute-start | bytes 737288 | tf_op jit(solution)/shard_map/ppermute | solution.py:516
  7.9 1.3 %collective-permute-start.2 = (f32[480,128]{1,0:T(8,128)S(1)}, f32[480,128]{1,0:T(8,128)S(1)}, u32[]{:S(2)}, u32[]{:S(2)}) collective-permute-start(f32[480,128]{1,0:T(8,128)S(1)} %get-tuple-element.11), channel_id=1, source_target_pairs={{0,24},{8,0},{16,8},{24,16},{1,25},{9,1},{17,9},{25,17},{2,26},{10... | collective-permute-start | bytes 737288 | tf_op jit(solution)/shard_map/ppermute | solution.py:516
  9.2 0.7 %multiply_reduce_fusion = f32[80]{0:T(128)S(1)} fusion(f32[4,80]{1,0:T(4,128)} %param.11), kind=kLoop, calls=%fused_computation.13 | loop fusion | flops 560 | bytes 1600 | tf_op jit(solution)/shard_map/reduce_sum | solution.py:586
  9.9 0.7 %broadcast_divide_fusion = f32[4,80]{1,0:T(4,128)S(1)} fusion(f32[4,80]{1,0:T(4,128)} %param.11, f32[80]{0:T(128)S(1)} %sqrt.8), kind=kLoop, calls=%fused_computation.14 | loop fusion | flops 320 | bytes 2880 | tf_op jit(solution)/shard_map/div | solution.py:586
  11.1 3.1 %collective-permute-done.refs_1_ = f32[480,128]{1,0:T(8,128)S(1)} collective-permute-done((f32[480,128]{1,0:T(8,128)S(1)}, f32[480,128]{1,0:T(8,128)S(1)}, u32[]{:S(2)}, u32[]{:S(2)}) %collective-permute-start) | collective-permute-done | bytes 245792 | tf_op jit(solution)/shard_map/ppermute | solution.py:516
  14.3 9.7 %collective-permute-done.1.refs_2_ = f32[480,128]{1,0:T(8,128)S(1)} collective-permute-done((f32[480,128]{1,0:T(8,128)S(1)}, f32[480,128]{1,0:T(8,128)S(1)}, u32[]{:S(2)}, u32[]{:S(2)}) %collective-permute-start.1) | collective-permute-done | bytes 245792 | tf_op jit(solution)/shard_map/ppermute | solution.py:516
  24.0 0.5 broadcast_in_dim.28.table_ref
  24.5 21.2 %sweep.1 = (f32[40,80]{1,0:T(8,128)S(1)}, f32[4,128]{1,0:T(4,128)S(1)}) custom-call(s32[1]{0:T(128)} %bitcast.place_ref, f32[80]{0:T(128)S(1)} %copy-done, f32[440,8,128]{2,1,0:T(8,128)S(1)} %broadcast_in_dim.28.table_ref, f32[480,128]{1,0:T(8,128)S(1)} %get-tuple-element.8.refs_0_, f32[480,128]{1,0:T(8,128)S(1)} %collective-permute-done.refs_1_, ...), custom_call_target="tpu_custom_call" | custom-call | tf_op jit(solution)/shard_map/sweep/pallas_call | solution.py:603
  46.0 5.8 %collective-permute-start.3 = (f32[1312]{0:T(1024)S(1)}, f32[1312]{0:T(1024)S(1)}, u32[]{:S(2)}, u32[]{:S(2)}) collective-permute-start(f32[1312]{0:T(1024)S(1)} %get-tuple-element.14), channel_id=1, source_target_pairs={{0,8},{8,16},{16,24},{24,0},{1,9},{9,17},{17,25},{25,1},{2,10},{10... | collective-permute-start | bytes 15752 | tf_op jit(solution)/shard_map/ppermute | solution.py:516
  51.8 1.1 %collective-permute-start.5 = (f32[1312]{0:T(1024)S(1)}, f32[1312]{0:T(1024)S(1)}, u32[]{:S(2)}, u32[]{:S(2)}) collective-permute-start(f32[1312]{0:T(1024)S(1)} %get-tuple-element.15), channel_id=1, source_target_pairs={{0,24},{8,0},{16,8},{24,16},{1,25},{9,1},{17,9},{25,17},{2,26},{10... | collective-permute-start | bytes 15752 | tf_op jit(solution)/shard_map/ppermute | solution.py:516
  52.9 0.5 collective-permute-start.4
  53.5 1.0 %collective-permute-done.3 = f32[1312]{0:T(1024)S(1)} collective-permute-done((f32[1312]{0:T(1024)S(1)}, f32[1312]{0:T(1024)S(1)}, u32[]{:S(2)}, u32[]{:S(2)}) %collective-permute-start.3) | collective-permute-done | bytes 5280 | tf_op jit(solution)/shard_map/ppermute | solution.py:516
  54.5 0.9 %collective-permute-done.5 = f32[1312]{0:T(1024)S(1)} collective-permute-done((f32[1312]{0:T(1024)S(1)}, f32[1312]{0:T(1024)S(1)}, u32[]{:S(2)}, u32[]{:S(2)}) %collective-permute-start.5) | collective-permute-done | bytes 5280 | tf_op jit(solution)/shard_map/ppermute | solution.py:516
  55.5 1.9 %collective-permute-done.4 = f32[1312]{0:T(1024)S(1)} collective-permute-done((f32[1312]{0:T(1024)S(1)}, f32[1312]{0:T(1024)S(1)}, u32[]{:S(2)}, u32[]{:S(2)}) %collective-permute-start.4) | collective-permute-done | bytes 5280 | tf_op jit(solution)/shard_map/ppermute | solution.py:516
  57.9 0.8 %collective-permute-done.6 = f32[10,80]{1,0:T(8,128)S(1)} collective-permute-done((f32[10,80]{1,0:T(8,128)S(1)}, f32[10,80]{1,0:T(8,128)S(1)}, u32[]{:S(2)}, u32[]{:S(2)}) %collective-permute-start.6) | collective-permute-done | bytes 3232 | tf_op jit(solution)/shard_map/ppermute | solution.py:528
  58.7 2.4 %collective-permute-start.9 = (f32[10,80]{1,0:T(8,128)S(1)}, f32[10,80]{1,0:T(8,128)S(1)}, u32[]{:S(2)}, u32[]{:S(2)}) collective-permute-start(f32[10,80]{1,0:T(8,128)S(1)} %add.84), channel_id=1, source_target_pairs={{0,6},{1,7},{2,4},{3,5},{4,2},{5,3},{6,0},{7,1},{8,14},{9,15},{10,... | collective-permute-start | bytes 9608 | tf_op jit(solution)/shard_map/ppermute | solution.py:528
  61.2 0.5 collective-permute-start.8
  61.7 0.5 collective-permute-start.7
  62.2 0.6 copy.15
  63.3 1.5 %collective-permute-done.8 = f32[10,80]{1,0:T(8,128)S(1)} collective-permute-done((f32[10,80]{1,0:T(8,128)S(1)}, f32[10,80]{1,0:T(8,128)S(1)}, u32[]{:S(2)}, u32[]{:S(2)}) %collective-permute-start.8) | collective-permute-done | bytes 3232 | tf_op jit(solution)/shard_map/ppermute | solution.py:528
  64.8 0.5 collective-permute-done.7
  65.4 0.7 %multiply_select_fusion = f32[10,80]{1,0:T(8,128)} fusion(f32[10,80]{1,0:T(8,128)S(1)} %copy-done.1, f32[10,80]{1,0:T(8,128)S(1)} %collective-permute-done.8, f32[10,80]{1,0:T(8,128)S(1)} %collective-permute-done.9, f32[10,80]{1,0:T(8,128)S(1)} %add.84, f32[10,80]{1,0:T(8,128)S(1)} %collective-permute-done.7, s32[10]{0:T(128)S(1)} %multiply_add_fusion), kind=kLoop, calls=%fused_computation.2 | loop fusion | flops 5600 | bytes 19240 | tf_op jit(solution)/shard_map/jit(_where)/select_n | solution.py:652
  (40 shorter events, 1.9 us)
Async XLA Ops:
  0.6 23.8 %copy-start = (f32[80]{0:T(128)S(1)}, f32[80]{0:T(128)}, u32[]{:S(2)}) copy-start(f32[80]{0:T(128)} %curve_ref.1) | copy-start | bytes 964
  2.2 12.1 %collective-permute-start = (f32[480,128]{1,0:T(8,128)S(1)}, f32[480,128]{1,0:T(8,128)S(1)}, u32[]{:S(2)}, u32[]{:S(2)}) collective-permute-start(f32[480,128]{1,0:T(8,128)S(1)} %get-tuple-element.9), channel_id=1, source_target_pairs={{0,8},{8,16},{16,24},{24,0},{1,9},{9,17},{17,25},{25,1},{2,10},{10... | collective-permute-start | bytes 737288 | tf_op jit(solution)/shard_map/ppermute | solution.py:516
  5.3 18.6 %collective-permute-start.1 = (f32[480,128]{1,0:T(8,128)S(1)}, f32[480,128]{1,0:T(8,128)S(1)}, u32[]{:S(2)}, u32[]{:S(2)}) collective-permute-start(f32[480,128]{1,0:T(8,128)S(1)} %get-tuple-element.10), channel_id=1, source_target_pairs={{0,16},{8,24},{16,0},{24,8},{1,17},{9,25},{17,1},{25,9},{2,18},{10... | collective-permute-start | bytes 737288 | tf_op jit(solution)/shard_map/ppermute | solution.py:516
  7.9 16.1 %collective-permute-start.2 = (f32[480,128]{1,0:T(8,128)S(1)}, f32[480,128]{1,0:T(8,128)S(1)}, u32[]{:S(2)}, u32[]{:S(2)}) collective-permute-start(f32[480,128]{1,0:T(8,128)S(1)} %get-tuple-element.11), channel_id=1, source_target_pairs={{0,24},{8,0},{16,8},{24,16},{1,25},{9,1},{17,9},{25,17},{2,26},{10... | collective-permute-start | bytes 737288 | tf_op jit(solution)/shard_map/ppermute | solution.py:516
  24.5 40.9 %copy-start.1 = (f32[10,80]{1,0:T(8,128)S(1)}, f32[10,80]{1,0:T(8,128)}, u32[]{:S(2)}) copy-start(f32[10,80]{1,0:T(8,128)} %refs_5_.1) | copy-start | bytes 9604
  46.0 8.4 %collective-permute-start.3 = (f32[1312]{0:T(1024)S(1)}, f32[1312]{0:T(1024)S(1)}, u32[]{:S(2)}, u32[]{:S(2)}) collective-permute-start(f32[1312]{0:T(1024)S(1)} %get-tuple-element.14), channel_id=1, source_target_pairs={{0,8},{8,16},{16,24},{24,0},{1,9},{9,17},{17,25},{25,1},{2,10},{10... | collective-permute-start | bytes 15752 | tf_op jit(solution)/shard_map/ppermute | solution.py:516
  51.8 3.7 %collective-permute-start.5 = (f32[1312]{0:T(1024)S(1)}, f32[1312]{0:T(1024)S(1)}, u32[]{:S(2)}, u32[]{:S(2)}) collective-permute-start(f32[1312]{0:T(1024)S(1)} %get-tuple-element.15), channel_id=1, source_target_pairs={{0,24},{8,0},{16,8},{24,16},{1,25},{9,1},{17,9},{25,17},{2,26},{10... | collective-permute-start | bytes 15752 | tf_op jit(solution)/shard_map/ppermute | solution.py:516
  52.9 4.5 %collective-permute-start.4 = (f32[1312]{0:T(1024)S(1)}, f32[1312]{0:T(1024)S(1)}, u32[]{:S(2)}, u32[]{:S(2)}) collective-permute-start(f32[1312]{0:T(1024)S(1)} %get-tuple-element.16), channel_id=1, source_target_pairs={{0,16},{8,24},{16,0},{24,8},{1,17},{9,25},{17,1},{25,9},{2,18},{10... | collective-permute-start | bytes 15752 | tf_op jit(solution)/shard_map/ppermute | solution.py:516
  57.5 1.2 %collective-permute-start.6 = (f32[10,80]{1,0:T(8,128)S(1)}, f32[10,80]{1,0:T(8,128)S(1)}, u32[]{:S(2)}, u32[]{:S(2)}) collective-permute-start(f32[10,80]{1,0:T(8,128)S(1)} %add_add_fusion), channel_id=1, source_target_pairs={{0,1},{1,0},{2,3},{3,2},{4,5},{5,4},{6,7},{7,6},{8,9},{9,8},{10,11... | collective-permute-start | bytes 9608 | tf_op jit(solution)/shard_map/ppermute | solution.py:528
  58.7 4.5 %collective-permute-start.9 = (f32[10,80]{1,0:T(8,128)S(1)}, f32[10,80]{1,0:T(8,128)S(1)}, u32[]{:S(2)}, u32[]{:S(2)}) collective-permute-start(f32[10,80]{1,0:T(8,128)S(1)} %add.84), channel_id=1, source_target_pairs={{0,6},{1,7},{2,4},{3,5},{4,2},{5,3},{6,0},{7,1},{8,14},{9,15},{10,... | collective-permute-start | bytes 9608 | tf_op jit(solution)/shard_map/ppermute | solution.py:528
  61.2 3.7 %collective-permute-start.8 = (f32[10,80]{1,0:T(8,128)S(1)}, f32[10,80]{1,0:T(8,128)S(1)}, u32[]{:S(2)}, u32[]{:S(2)}) collective-permute-start(f32[10,80]{1,0:T(8,128)S(1)} %add.84), channel_id=1, source_target_pairs={{0,4},{1,5},{2,6},{3,7},{4,0},{5,1},{6,2},{7,3},{8,12},{9,13},{10,... | collective-permute-start | bytes 9608 | tf_op jit(solution)/shard_map/ppermute | solution.py:528
  61.7 3.7 %collective-permute-start.7 = (f32[10,80]{1,0:T(8,128)S(1)}, f32[10,80]{1,0:T(8,128)S(1)}, u32[]{:S(2)}, u32[]{:S(2)}) collective-permute-start(f32[10,80]{1,0:T(8,128)S(1)} %add.84), channel_id=1, source_target_pairs={{0,2},{1,3},{2,0},{3,1},{4,6},{5,7},{6,4},{7,5},{8,10},{9,11},{10,... | collective-permute-start | bytes 9608 | tf_op jit(solution)/shard_map/ppermute | solution.py:528
